TPU v7x, 256 devices: a whole 4x4x8 slice. The times are simulated.
256 devices in a mesh: ctx: 64 (over z_lo, y, x, core), head: 4 (over z_hi).
Axes of the slice: x: 4, y: 4, z: 8 (z_hi: 4, z_lo: 2; z = z_hi * 2 + z_lo), core: 2. Of those that a mesh axis runs over, the one named last changes fastest.
Arguments:
- queries: bfloat16 [12288, 4096], P('ctx', 'head'), may hold values from -6 to 6
- keys: bfloat16 [12288, 1024], P('ctx', 'head'), may hold values from -6 to 6
- values: bfloat16 [12288, 1024], P('ctx', 'head'), may hold values from -6 to 6
- retrieval: int32 [32], replicated, may hold values 0 or 1
- spans: int32 [2, 32], replicated, may hold values from 64 to 4096, as said below
- out_weight: bfloat16 [4096, 4096], P(None, 'head'), may hold values from -0.09375 to 0.09375
Outputs:
- layer_out: bfloat16 [12288, 4096], P('ctx', 'head')
Inputs may be any that keep to these rules, and one draw needn't show every extreme that they name: `spans`: row 0 lies within 64 to 128, row 1 within 2048 to 4096; some head has exactly 128 sink tokens and some head exactly 4096 recent tokens.
All inputs are finite; a program needn't handle non-finite values.
Results may differ from a plain program's by a relative error of at most 0.0075.
Values may be sent and summed in bfloat16 or wider, within the bound.
No kernel may reach another device: no remote copies, remote signals or barrier semaphores. Data moves between devices by JAX's collectives and lax.ppermute only.
A program may use at most 192 MiB of HBM per device.

v0:
```python
import functools

import jax
import jax.numpy as jnp
from jax import lax
from jax.experimental import pallas as pl
from jax.experimental.pallas import tpu as pltpu
from jax.sharding import PartitionSpec as P


HD = 128
ROWS = 192
SEQ = 12288
TILE = 768
TILES = SEQ // TILE
HEADS = 32
STRIP = 32
GROUP = 4
NEG = -1e30


def ctx_pairs(flip):
    return [(i, i ^ flip) for i in range(64)]


def by_core(flip0, flip1):
    return [(i, i ^ (flip1 if i % 2 else flip0)) for i in range(64)]


def to_class(turn):
    return [(i, ((i % 2) ^ turn) * 32 + (i % 32) // 2 * 2 + i // 32) for i in range(64)]


CORE = ctx_pairs(1)
MIRROR = ctx_pairs(63)
KEY_STEPS = (by_core(2, 8), by_core(6, 24), by_core(8, 2), by_core(24, 6))
VALUE_STEPS = (KEY_STEPS[1], KEY_STEPS[0], KEY_STEPS[3], KEY_STEPS[2])


def head_pairs(flip0, flip1):
    flip = lambda i: flip1 if (i // 4) % 2 else flip0
    return [(i, i ^ flip(i)) for i in range(256)]


HEAD_STEPS = (head_pairs(1, 3), head_pairs(3, 1))


def swap(a, pairs):
    return lax.ppermute(a, "ctx", pairs)


def head_swap(a, step):
    return lax.ppermute(a, ("ctx", "head"), HEAD_STEPS[step])


def attention_kernel(mirrored, table, q_ref, *refs):
    pieces, out, scratch = refs[:8], refs[8], refs[9:]
    kbuf, vbuf, qbuf, acc, top, tot, gaps, sa, sb, pa, pb, fa, fb, items = scratch
    at = lax.axis_index("ctx")
    half, pos = at // 32, at % 32
    first_head = (2 * lax.axis_index("head") + half) * GROUP
    y, x, core = pos // 8, (pos // 2) % 4, pos % 2

    for s in range(8):
        value, other, late = s // 4, (s // 2) % 2, s % 2
        dst = vbuf if value else kbuf
        f1, f3 = (3, 1) if value else (1, 3)
        z = core ^ other
        for e in range(16):
            a = (f1 * ((e // 2) % 2)) ^ (f3 * ((e // 4) % 2))
            b = (f1 * (e // 8)) ^ (f3 * late)
            fx, fy = jnp.where(z == 0, a, b), jnp.where(z == 0, b, a)
            block = z * 32 + (y ^ fy) * 8 + (x ^ fx) * 2 + (half ^ (e % 2))
            dst[pl.ds(pl.multiple_of(block * ROWS, ROWS), ROWS)] = pieces[s][e]
    for j in range(GROUP):
        qbuf[j] = q_ref[:, j * HD : (j + 1) * HD]
    acc[...] = jnp.zeros_like(acc)
    tot[...] = jnp.zeros_like(tot)
    top[...] = jnp.full_like(top, NEG)
    gaps[...] = lax.broadcasted_iota(jnp.int32, gaps.shape, 0) - lax.broadcasted_iota(
        jnp.int32, gaps.shape, 1
    )

    row0 = (63 - at if mirrored else at) * ROWS

    def reach_of(u):
        return jnp.where(table[first_head + u] > 0, SEQ + ROWS, table[2 * HEADS + first_head + u])

    def list_unit(u, counts):
        reach = reach_of(u)
        low = jnp.maximum(row0 - reach + 1, 0) // TILE
        diag = row0 // TILE

        def put(t, counts):
            edge = (t == diag) | (t * TILE < row0 + ROWS - reach)
            kind = jnp.where(edge, 0, 1)
            n = jnp.where(edge, counts[0], counts[1])
            items[kind, n] = u * TILES + t
            return counts[0] + 1 - kind, counts[1] + kind

        counts = lax.cond(low > 0, lambda c: put(0, c), lambda c: c, counts)
        return lax.fori_loop(low, diag + 1, put, counts)

    masked, plain = lax.fori_loop(0, GROUP, list_unit, (0, 0))
    odd = plain % 2
    items[0, masked] = items[1, jnp.maximum(plain - 1, 0)]
    masked, plain = masked + odd, plain - odd
    items[0, masked] = items[0, 0]
    items[0, masked + 1] = items[0, 0]
    items[1, plain] = 0

    factor = HD ** (-0.5) * 1.4426950408889634

    def span(t):
        return pl.ds(pl.multiple_of(t * TILE, TILE), TILE)

    def score(item, s_ref):
        s_ref[...] = lax.dot_general(
            qbuf[item // TILES],
            kbuf[span(item % TILES)],
            (((1,), (1,)), ((), ())),
            preferred_element_type=jnp.float32,
        )

    def soften(item, s_ref, p_ref, f_ref, use_mask, live):
        u, t = item // TILES, item % TILES
        if use_mask:
            shift = t * TILE - row0
            first = jnp.where(live, shift, SEQ * 2)
            last = shift + reach_of(u)
            col = lax.broadcasted_iota(jnp.int32, (STRIP, TILE), 1)
            sink = col < table[HEADS + first_head + u] - t * TILE
        for r in range(0, ROWS, STRIP):
            rows = pl.ds(r, STRIP)
            s = s_ref[rows]
            if use_mask:
                gap = gaps[rows]
                s = jnp.where((gap >= first) & ((gap < last) | sink), s, NEG)
            high = jnp.max(s, axis=1, keepdims=True)
            old = top[u, rows]
            new = jnp.maximum(old, high)
            fade = jnp.exp2((old - new) * factor)
            base = new * factor
            part = None
            for n in range(TILE // HD):
                cols = pl.ds(n * HD, HD)
                p = jnp.exp2(s[:, n * HD : (n + 1) * HD] * factor - base)
                p_ref[rows, cols] = p.astype(jnp.bfloat16)
                part = p if part is None else part + p
            tot[u, rows] = tot[u, rows] * fade + part
            top[u, rows] = new
            f_ref[rows] = fade

    def gather_values(item, p_ref, f_ref):
        u = item // TILES
        pv = jnp.dot(p_ref[...], vbuf[span(item % TILES)], preferred_element_type=jnp.float32)
        acc[u] = acc[u] * f_ref[...] + pv

    def run(kind, count, use_mask):
        pb[...] = jnp.zeros_like(pb)
        fb[...] = jnp.ones_like(fb)
        score(items[kind, 0], sa)

        def two(k, before):
            i = 2 * k
            now, then, later = items[kind, i], items[kind, i + 1], items[kind, i + 2]
            score(then, sb)
            gather_values(before, pb, fb)
            soften(now, sa, pa, fa, use_mask, True)
            score(later, sa)
            gather_values(now, pa, fa)
            soften(then, sb, pb, fb, use_mask, i + 1 < count)
            return then

        before = lax.fori_loop(0, (count + 1) // 2, two, items[kind, 0])
        gather_values(before, pb, fb)

    run(0, masked, True)
    run(1, plain, False)

    for j in range(GROUP):
        total = jnp.sum(tot[j], axis=1, keepdims=True)
        out[:, j * HD : (j + 1) * HD] = (acc[j] / total).astype(jnp.bfloat16)


def attention(mirrored, table, q, pieces):
    out = jax.ShapeDtypeStruct((ROWS, GROUP * HD), jnp.bfloat16)
    vmem = pl.BlockSpec(memory_space=pltpu.VMEM)
    state = pltpu.VMEM((GROUP, ROWS, HD), jnp.float32)
    return pl.pallas_call(
        functools.partial(attention_kernel, mirrored),
        out_shape=out,
        in_specs=[pl.BlockSpec(memory_space=pltpu.SMEM)] + [vmem] * 9,
        out_specs=vmem,
        scratch_shapes=[
            pltpu.VMEM((SEQ, HD), jnp.bfloat16),
            pltpu.VMEM((SEQ, HD), jnp.bfloat16),
            pltpu.VMEM((GROUP, ROWS, HD), jnp.bfloat16),
            state,
            state,
            state,
            pltpu.VMEM((ROWS, TILE), jnp.int32),
            pltpu.VMEM((ROWS, TILE), jnp.float32),
            pltpu.VMEM((ROWS, TILE), jnp.float32),
            pltpu.VMEM((ROWS, TILE), jnp.bfloat16),
            pltpu.VMEM((ROWS, TILE), jnp.bfloat16),
            pltpu.VMEM((ROWS, HD), jnp.float32),
            pltpu.VMEM((ROWS, HD), jnp.float32),
            pltpu.SMEM((2, GROUP * (TILES + 2)), jnp.int32),
        ],
        compiler_params=pltpu.CompilerParams(vmem_limit_bytes=20 * 2**20),
        cost_estimate=pl.CostEstimate(
            flops=4_000_000_000, bytes_accessed=8_000_000, transcendentals=7_000_000
        ),
    )(table, q, *pieces)


def project_kernel(sources, *refs):
    pieces, w, before, out = refs[: len(sources)], refs[len(sources)], refs[len(sources) + 1 : -1], refs[-1]
    width = GROUP * HD
    h, at = lax.axis_index("head"), lax.axis_index("ctx")
    total = before[0][...] if before else None
    for piece, (part, flips) in zip(pieces, sources):
        for n, (flip0, flip1) in enumerate(flips):
            group = h ^ jnp.where(at % 2 == 0, flip0, flip1)
            start = (2 * group + ((at // 32) ^ part)) * width
            rows = w[pl.ds(pl.multiple_of(start, width), width)]
            value = piece[n] if len(flips) > 1 else piece[...]
            term = jnp.dot(value, rows, preferred_element_type=jnp.float32)
            total = term if total is None else total + term
    out[...] = total.astype(out.dtype)


def project(sources, dtype, pieces, w, *before):
    vmem = pl.BlockSpec(memory_space=pltpu.VMEM)
    count = sum(len(flips) for _, flips in sources)
    return pl.pallas_call(
        functools.partial(project_kernel, sources),
        out_shape=jax.ShapeDtypeStruct((ROWS, w.shape[1]), dtype),
        in_specs=[vmem] * (len(pieces) + 1 + len(before)),
        out_specs=vmem,
        compiler_params=pltpu.CompilerParams(vmem_limit_bytes=16 * 2**20),
        cost_estimate=pl.CostEstimate(
            flops=200_000_000 * count, bytes_accessed=2_000_000 * count, transcendentals=0
        ),
    )(*pieces, w, *before)


SAME, NEAR, FAR = ((0, 0),), ((1, 3),), ((3, 1), (2, 2))


def layer(queries, keys, values, retrieval, spans, out_weight):
    at = lax.axis_index("ctx")
    half = at // 32
    width = GROUP * HD
    core = at % 2
    kv_both = jnp.stack([keys, values])
    kv_a = swap(lax.dynamic_slice_in_dim(kv_both, core * HD, HD, axis=2), to_class(0))
    kv_b = swap(lax.dynamic_slice_in_dim(kv_both, (1 - core) * HD, HD, axis=2), to_class(1))
    q_mine = lax.dynamic_slice_in_dim(queries, half * width, width, axis=1)
    q_out = lax.dynamic_slice_in_dim(queries, (1 - half) * width, width, axis=1)
    k = jnp.stack([kv_a[0], kv_b[0]])
    v = jnp.stack([kv_a[1], kv_b[1]])
    for step in range(3):
        k_got, v_got = swap(k, KEY_STEPS[step]), swap(v, VALUE_STEPS[step])
        k, v = jnp.concatenate([k, k_got]), jnp.concatenate([v, v_got])
    table = jnp.concatenate([retrieval, spans[0], spans[1]])
    k, v, table, q_out = lax.optimization_barrier((k, v, table, q_out))
    k_last, v_last = swap(k, KEY_STEPS[3]), swap(v, VALUE_STEPS[3])
    q_in = swap(q_out, MIRROR)
    pieces = (k, k_last, swap(k, CORE), swap(k_last, CORE))
    pieces += (v, v_last, swap(v, CORE), swap(v_last, CORE))
    mine = attention(False, table, q_mine, pieces)
    mine_near = head_swap(mine, 0)
    q_in, _ = lax.optimization_barrier((q_in, mine))
    other = attention(True, table, q_in, pieces)
    theirs = swap(other, MIRROR)
    mine_far = head_swap(jnp.stack([mine, mine_near]), 1)
    total = project(((0, SAME), (0, NEAR)), jnp.float32, (mine, mine_near), out_weight)
    their_near = head_swap(theirs, 0)
    their_far = head_swap(jnp.stack([theirs, their_near]), 1)
    total = project(((0, FAR), (1, SAME)), jnp.float32, (mine_far, theirs), out_weight, total)
    return project(
        ((1, NEAR), (1, FAR)), jnp.bfloat16, (their_near, their_far), out_weight, total
    )


def solution(mesh):
    in_specs = (P("ctx", "head"), P("ctx", "head"), P("ctx", "head"), P(), P(), P(None, "head"))
    out_specs = P("ctx", "head")
    return jax.shard_map(layer, mesh=mesh, in_specs=in_specs, out_specs=out_specs, check_vma=False)
```

profile of v0, /device:TPU:1, one launch (start us, length us, event | category | flops | bytes accessed | tf_op | source)
XLA Modules:
  0.0 113.3 jit_solution(921113767564355417)
XLA Ops:
  0.9 3.3 %collective-permute-start.1 = (bf16[2,192,128]{2,1,0:T(8,128)(2,1)S(1)}, bf16[2,192,128]{2,1,0:T(8,128)(2,1)S(1)}, u32[]{:S(2)}, u32[]{:S(2)}) collective-permute-start(bf16[2,192,128]{2,1,0:T(8,128)(2,1)S(1)} %get-tuple-element.17), channel_id=1, source_target_pairs={{0,128},{4,0},{8,136},{12,8},{16,144},{20,16},{24,152},{28,24},{32... | collective-permute-start | bytes 294920 | tf_op jit(solution)/shard_map/ppermute | solution.py:49
  4.2 1.9 %collective-permute-start = (bf16[2,192,128]{2,1,0:T(8,128)(2,1)S(1)}, bf16[2,192,128]{2,1,0:T(8,128)(2,1)S(1)}, u32[]{:S(2)}, u32[]{:S(2)}) collective-permute-start(bf16[2,192,128]{2,1,0:T(8,128)(2,1)S(1)} %get-tuple-element.18), channel_id=1, source_target_pairs={{0,0},{4,128},{8,8},{12,136},{16,16},{20,144},{24,24},{28,152},{32... | collective-permute-start | bytes 294920 | tf_op jit(solution)/shard_map/ppermute | solution.py:49
  6.9 1.0 constant_dynamic-slice_fusion
  8.7 1.4 %collective-permute-done = bf16[2,192,128]{2,1,0:T(8,128)(2,1)S(1)} collective-permute-done((bf16[2,192,128]{2,1,0:T(8,128)(2,1)S(1)}, bf16[2,192,128]{2,1,0:T(8,128)(2,1)S(1)}, u32[]{:S(2)}, u32[]{:S(2)}) %collective-permute-start) | collective-permute-done | bytes 98336 | tf_op jit(solution)/shard_map/ppermute | solution.py:49
  10.2 1.2 %collective-permute-start.5 = (bf16[2,192,128]{2,1,0:T(8,128)(2,1)S(1)}, bf16[2,192,128]{2,1,0:T(8,128)(2,1)S(1)}, u32[]{:S(2)}, u32[]{:S(2)}) collective-permute-start(bf16[2,192,128]{2,1,0:T(8,128)(2,1)S(1)} %pad_maximum_fusion.7), channel_id=1, source_target_pairs={{0,24},{4,100},{8,16},{12,108},{16,8},{20,116},{24,0},{28,124},{32... | collective-permute-start | bytes 294920 | tf_op jit(solution)/shard_map/ppermute | solution.py:49
  11.5 3.4 %collective-permute-done.5 = bf16[2,192,128]{2,1,0:T(8,128)(2,1)S(1)} collective-permute-done((bf16[2,192,128]{2,1,0:T(8,128)(2,1)S(1)}, bf16[2,192,128]{2,1,0:T(8,128)(2,1)S(1)}, u32[]{:S(2)}, u32[]{:S(2)}) %collective-permute-start.5) | collective-permute-done | bytes 98336 | tf_op jit(solution)/shard_map/ppermute | solution.py:49
  15.1 1.8 %collective-permute-start.3 = (bf16[4,192,128]{2,1,0:T(8,128)(2,1)S(1)}, bf16[4,192,128]{2,1,0:T(8,128)(2,1)S(1)}, u32[]{:S(2)}, u32[]{:S(2)}) collective-permute-start(bf16[4,192,128]{2,1,0:T(8,128)(2,1)S(1)} %pad_maximum_fusion.4), channel_id=1, source_target_pairs={{0,24},{4,100},{8,16},{12,108},{16,8},{20,116},{24,0},{28,124},{32... | collective-permute-start | bytes 589832 | tf_op jit(solution)/shard_map/ppermute | solution.py:49
  17.0 2.9 %collective-permute-done.6 = bf16[4,192,128]{2,1,0:T(8,128)(2,1)S(1)} collective-permute-done((bf16[4,192,128]{2,1,0:T(8,128)(2,1)S(1)}, bf16[4,192,128]{2,1,0:T(8,128)(2,1)S(1)}, u32[]{:S(2)}, u32[]{:S(2)}) %collective-permute-start.6) | collective-permute-done | bytes 196640 | tf_op jit(solution)/shard_map/ppermute | solution.py:49
  22.3 5.9 %collective-permute-done.7 = bf16[8,192,128]{2,1,0:T(8,128)(2,1)S(1)} collective-permute-done((bf16[8,192,128]{2,1,0:T(8,128)(2,1)S(1)}, bf16[8,192,128]{2,1,0:T(8,128)(2,1)S(1)}, u32[]{:S(2)}, u32[]{:S(2)}) %collective-permute-start.7) | collective-permute-done | bytes 393248 | tf_op jit(solution)/shard_map/ppermute | solution.py:49
  28.4 2.1 %collective-permute-start.9 = (bf16[16,192,128]{2,1,0:T(8,128)(2,1)S(1)}, bf16[16,192,128]{2,1,0:T(8,128)(2,1)S(1)}, u32[]{:S(2)}, u32[]{:S(2)}) collective-permute-start(bf16[16,192,128]{2,1,0:T(8,128)(2,1)S(1)} %constant_dynamic-update-slice_fusion.refs_0_), channel_id=1, source_target_pairs={{0,96},{4,28},{8,104},{12,20},{16,112},{20,12},{24,120},{28,4},{32... | collective-permute-start | bytes 2359304 | tf_op jit(solution)/shard_map/ppermute | solution.py:49
  30.5 3.0 %collective-permute-start.10 = (bf16[16,192,128]{2,1,0:T(8,128)(2,1)S(1)}, bf16[16,192,128]{2,1,0:T(8,128)(2,1)S(1)}, u32[]{:S(2)}, u32[]{:S(2)}) collective-permute-start(bf16[16,192,128]{2,1,0:T(8,128)(2,1)S(1)} %constant_dynamic-update-slice_fusion.refs_0_), channel_id=1, source_target_pairs={{0,4},{4,0},{8,12},{12,8},{16,20},{20,16},{24,28},{28,24},{32,36},... | collective-permute-start | bytes 2359304 | tf_op jit(solution)/shard_map/ppermute | solution.py:49
  33.5 7.3 %collective-permute-done.9.refs_1_ = bf16[16,192,128]{2,1,0:T(8,128)(2,1)S(1)} collective-permute-done((bf16[16,192,128]{2,1,0:T(8,128)(2,1)S(1)}, bf16[16,192,128]{2,1,0:T(8,128)(2,1)S(1)}, u32[]{:S(2)}, u32[]{:S(2)}) %collective-permute-start.9) | collective-permute-done | bytes 786464 | tf_op jit(solution)/shard_map/ppermute | solution.py:49
  40.8 3.0 %collective-permute-start.11 = (bf16[16,192,128]{2,1,0:T(8,128)(2,1)S(1)}, bf16[16,192,128]{2,1,0:T(8,128)(2,1)S(1)}, u32[]{:S(2)}, u32[]{:S(2)}) collective-permute-start(bf16[16,192,128]{2,1,0:T(8,128)(2,1)S(1)} %collective-permute-done.9.refs_1_), channel_id=1, source_target_pairs={{0,4},{4,0},{8,12},{12,8},{16,20},{20,16},{24,28},{28,24},{32,36},... | collective-permute-start | bytes 2359304 | tf_op jit(solution)/shard_map/ppermute | solution.py:49
  43.8 1.5 %collective-permute-start.14 = (bf16[16,192,128]{2,1,0:T(8,128)(2,1)S(1)}, bf16[16,192,128]{2,1,0:T(8,128)(2,1)S(1)}, u32[]{:S(2)}, u32[]{:S(2)}) collective-permute-start(bf16[16,192,128]{2,1,0:T(8,128)(2,1)S(1)} %collective-permute-done.12.refs_5_), channel_id=1, source_target_pairs={{0,4},{4,0},{8,12},{12,8},{16,20},{20,16},{24,28},{28,24},{32,36},... | collective-permute-start | bytes 2359304 | tf_op jit(solution)/shard_map/ppermute | solution.py:49
  45.3 6.3 %collective-permute-start.8 = (bf16[192,512]{1,0:T(8,128)(2,1)S(1)}, bf16[192,512]{1,0:T(8,128)(2,1)S(1)}, u32[]{:S(2)}, u32[]{:S(2)}) collective-permute-start(bf16[192,512]{1,0:T(8,128)(2,1)S(1)} %get-tuple-element.11), channel_id=1, source_target_pairs={{0,252},{4,248},{8,244},{12,240},{16,236},{20,232},{24,228},{28,22... | collective-permute-start | bytes 589832 | tf_op jit(solution)/shard_map/ppermute | solution.py:49
  51.6 3.8 %shard_map.64.refs_0_ = bf16[192,512]{1,0:T(8,128)(2,1)S(1)} custom-call(s32[96]{0:T(128)S(1)} %pad_add_fusion.table, bf16[192,512]{1,0:T(8,128)(2,1)S(1)} %get-tuple-element.15.q_ref, bf16[16,192,128]{2,1,0:T(8,128)(2,1)S(1)} %constant_dynamic-update-slice_fusion.refs_0_, bf16[16,192,128]{2,1,0:T(8,128)(2,1)S(1)} %collective-permute-done.9.refs_1_, ...), custom_call_target="tpu_custom_call" | custom-call | flops 4000000000 | bytes 8000000 | tf_op jit(solution)/shard_map/pallas_call | solution.py:190
  56.4 18.5 %shard_map.65 = bf16[192,512]{1,0:T(8,128)(2,1)S(1)} custom-call(s32[96]{0:T(128)S(1)} %pad_add_fusion.table, bf16[192,512]{1,0:T(8,128)(2,1)S(1)} %collective-permute-done.8.q_ref, bf16[16,192,128]{2,1,0:T(8,128)(2,1)S(1)} %constant_dynamic-update-slice_fusion.refs_0_, bf16[16,192,128]{2,1,0:T(8,128)(2,1)S(1)} %collective-permute-done.9.refs_1_, ...), custom_call_target="tpu_custom_call" | custom-call | flops 4000000000 | bytes 8000000 | tf_op jit(solution)/shard_map/pallas_call | solution.py:190
  75.0 4.3 %collective-permute-start.18 = (bf16[192,512]{1,0:T(8,128)(2,1)S(1)}, bf16[192,512]{1,0:T(8,128)(2,1)S(1)}, u32[]{:S(2)}, u32[]{:S(2)}) collective-permute-start(bf16[192,512]{1,0:T(8,128)(2,1)S(1)} %shard_map.64.refs_0_), channel_id=1, source_target_pairs={{0,1},{1,0},{2,3},{3,2},{4,7},{5,6},{6,5},{7,4},{8,9},{9,8},{10,11... | collective-permute-start | bytes 589832 | tf_op jit(solution)/shard_map/ppermute | solution.py:53
  79.3 9.2 %collective-permute-done.15.refs_1_ = bf16[192,512]{1,0:T(8,128)(2,1)S(1)} collective-permute-done((bf16[192,512]{1,0:T(8,128)(2,1)S(1)}, bf16[192,512]{1,0:T(8,128)(2,1)S(1)}, u32[]{:S(2)}, u32[]{:S(2)}) %collective-permute-start.15) | collective-permute-done | bytes 196640 | tf_op jit(solution)/shard_map/ppermute | solution.py:49
  88.5 1.4 %collective-permute-start.19 = (bf16[2,192,512]{2,1,0:T(8,128)(2,1)S(1)}, bf16[2,192,512]{2,1,0:T(8,128)(2,1)S(1)}, u32[]{:S(2)}, u32[]{:S(2)}) collective-permute-start(bf16[2,192,512]{2,1,0:T(8,128)(2,1)S(1)} %pad_maximum_fusion.3), channel_id=1, source_target_pairs={{0,3},{1,2},{2,1},{3,0},{4,5},{5,4},{6,7},{7,6},{8,11},{9,10},{10,... | collective-permute-start | bytes 1179656 | tf_op jit(solution)/shard_map/ppermute | solution.py:53
  90.0 9.5 %collective-permute-done.16.refs_0_ = bf16[192,512]{1,0:T(8,128)(2,1)S(1)} collective-permute-done((bf16[192,512]{1,0:T(8,128)(2,1)S(1)}, bf16[192,512]{1,0:T(8,128)(2,1)S(1)}, u32[]{:S(2)}, u32[]{:S(2)}) %collective-permute-start.16) | collective-permute-done | bytes 196640 | tf_op jit(solution)/shard_map/ppermute | solution.py:53
  100.2 2.0 %collective-permute-done.19.refs_0_ = bf16[2,192,512]{2,1,0:T(8,128)(2,1)S(1)} collective-permute-done((bf16[2,192,512]{2,1,0:T(8,128)(2,1)S(1)}, bf16[2,192,512]{2,1,0:T(8,128)(2,1)S(1)}, u32[]{:S(2)}, u32[]{:S(2)}) %collective-permute-start.19) | collective-permute-done | bytes 393248 | tf_op jit(solution)/shard_map/ppermute | solution.py:53
  103.1 8.7 %collective-permute-done.17.refs_1_ = bf16[2,192,512]{2,1,0:T(8,128)(2,1)S(1)} collective-permute-done((bf16[2,192,512]{2,1,0:T(8,128)(2,1)S(1)}, bf16[2,192,512]{2,1,0:T(8,128)(2,1)S(1)}, u32[]{:S(2)}, u32[]{:S(2)}) %collective-permute-start.17) | collective-permute-done | bytes 393248 | tf_op jit(solution)/shard_map/ppermute | solution.py:53
  111.8 1.6 %shard_map.68 = bf16[192,1024]{1,0:T(8,128)(2,1)} custom-call(bf16[192,512]{1,0:T(8,128)(2,1)S(1)} %collective-permute-done.16.refs_0_, bf16[2,192,512]{2,1,0:T(8,128)(2,1)S(1)} %collective-permute-done.17.refs_1_, bf16[4096,1024]{1,0:T(8,128)(2,1)S(1)} %bitcast.11, f32[192,1024]{1,0:T(8,128)S(1)} %shard_map.67.refs_3_), custom_call_target="tpu_custom_call" | custom-call | flops 600000000 | bytes 6000000 | tf_op jit(solution)/shard_map/pallas_call | solution.py:237
  (46 shorter events, 7.9 us)
Async XLA Ops:
  0.9 9.2 %collective-permute-start.1 = (bf16[2,192,128]{2,1,0:T(8,128)(2,1)S(1)}, bf16[2,192,128]{2,1,0:T(8,128)(2,1)S(1)}, u32[]{:S(2)}, u32[]{:S(2)}) collective-permute-start(bf16[2,192,128]{2,1,0:T(8,128)(2,1)S(1)} %get-tuple-element.17), channel_id=1, source_target_pairs={{0,128},{4,0},{8,136},{12,8},{16,144},{20,16},{24,152},{28,24},{32... | collective-permute-start | bytes 294920 | tf_op jit(solution)/shard_map/ppermute | solution.py:49
  4.2 5.9 %collective-permute-start = (bf16[2,192,128]{2,1,0:T(8,128)(2,1)S(1)}, bf16[2,192,128]{2,1,0:T(8,128)(2,1)S(1)}, u32[]{:S(2)}, u32[]{:S(2)}) collective-permute-start(bf16[2,192,128]{2,1,0:T(8,128)(2,1)S(1)} %get-tuple-element.18), channel_id=1, source_target_pairs={{0,0},{4,128},{8,8},{12,136},{16,16},{20,144},{24,24},{28,152},{32... | collective-permute-start | bytes 294920 | tf_op jit(solution)/shard_map/ppermute | solution.py:49
  10.2 4.8 %collective-permute-start.5 = (bf16[2,192,128]{2,1,0:T(8,128)(2,1)S(1)}, bf16[2,192,128]{2,1,0:T(8,128)(2,1)S(1)}, u32[]{:S(2)}, u32[]{:S(2)}) collective-permute-start(bf16[2,192,128]{2,1,0:T(8,128)(2,1)S(1)} %pad_maximum_fusion.7), channel_id=1, source_target_pairs={{0,24},{4,100},{8,16},{12,108},{16,8},{20,116},{24,0},{28,124},{32... | collective-permute-start | bytes 294920 | tf_op jit(solution)/shard_map/ppermute | solution.py:49
  11.4 3.7 %collective-permute-start.2 = (bf16[2,192,128]{2,1,0:T(8,128)(2,1)S(1)}, bf16[2,192,128]{2,1,0:T(8,128)(2,1)S(1)}, u32[]{:S(2)}, u32[]{:S(2)}) collective-permute-start(bf16[2,192,128]{2,1,0:T(8,128)(2,1)S(1)} %pad_maximum_fusion.6), channel_id=1, source_target_pairs={{0,8},{4,36},{8,0},{12,44},{16,24},{20,52},{24,16},{28,60},{32,40}... | collective-permute-start | bytes 294920 | tf_op jit(solution)/shard_map/ppermute | solution.py:49
  15.0 4.9 %collective-permute-start.6 = (bf16[4,192,128]{2,1,0:T(8,128)(2,1)S(1)}, bf16[4,192,128]{2,1,0:T(8,128)(2,1)S(1)}, u32[]{:S(2)}, u32[]{:S(2)}) collective-permute-start(bf16[4,192,128]{2,1,0:T(8,128)(2,1)S(1)} %pad_maximum_fusion.5), channel_id=1, source_target_pairs={{0,8},{4,36},{8,0},{12,44},{16,24},{20,52},{24,16},{28,60},{32,40}... | collective-permute-start | bytes 589832 | tf_op jit(solution)/shard_map/ppermute | solution.py:49
  15.1 6.1 %collective-permute-start.3 = (bf16[4,192,128]{2,1,0:T(8,128)(2,1)S(1)}, bf16[4,192,128]{2,1,0:T(8,128)(2,1)S(1)}, u32[]{:S(2)}, u32[]{:S(2)}) collective-permute-start(bf16[4,192,128]{2,1,0:T(8,128)(2,1)S(1)} %pad_maximum_fusion.4), channel_id=1, source_target_pairs={{0,24},{4,100},{8,16},{12,108},{16,8},{20,116},{24,0},{28,124},{32... | collective-permute-start | bytes 589832 | tf_op jit(solution)/shard_map/ppermute | solution.py:49
  19.9 8.2 %collective-permute-start.7 = (bf16[8,192,128]{2,1,0:T(8,128)(2,1)S(1)}, bf16[8,192,128]{2,1,0:T(8,128)(2,1)S(1)}, u32[]{:S(2)}, u32[]{:S(2)}) collective-permute-start(bf16[8,192,128]{2,1,0:T(8,128)(2,1)S(1)} %pad_maximum_fusion.1), channel_id=1, source_target_pairs={{0,96},{4,28},{8,104},{12,20},{16,112},{20,12},{24,120},{28,4},{32... | collective-permute-start | bytes 1179656 | tf_op jit(solution)/shard_map/ppermute | solution.py:49
  21.3 7.0 %collective-permute-start.4 = (bf16[8,192,128]{2,1,0:T(8,128)(2,1)S(1)}, bf16[8,192,128]{2,1,0:T(8,128)(2,1)S(1)}, u32[]{:S(2)}, u32[]{:S(2)}) collective-permute-start(bf16[8,192,128]{2,1,0:T(8,128)(2,1)S(1)} %pad_maximum_fusion), channel_id=1, source_target_pairs={{0,32},{4,12},{8,40},{12,4},{16,48},{20,28},{24,56},{28,20},{32,0}... | collective-permute-start | bytes 1179656 | tf_op jit(solution)/shard_map/ppermute | solution.py:49
  28.4 12.4 %collective-permute-start.9 = (bf16[16,192,128]{2,1,0:T(8,128)(2,1)S(1)}, bf16[16,192,128]{2,1,0:T(8,128)(2,1)S(1)}, u32[]{:S(2)}, u32[]{:S(2)}) collective-permute-start(bf16[16,192,128]{2,1,0:T(8,128)(2,1)S(1)} %constant_dynamic-update-slice_fusion.refs_0_), channel_id=1, source_target_pairs={{0,96},{4,28},{8,104},{12,20},{16,112},{20,12},{24,120},{28,4},{32... | collective-permute-start | bytes 2359304 | tf_op jit(solution)/shard_map/ppermute | solution.py:49
  30.5 13.3 %collective-permute-start.12 = (bf16[16,192,128]{2,1,0:T(8,128)(2,1)S(1)}, bf16[16,192,128]{2,1,0:T(8,128)(2,1)S(1)}, u32[]{:S(2)}, u32[]{:S(2)}) collective-permute-start(bf16[16,192,128]{2,1,0:T(8,128)(2,1)S(1)} %constant_dynamic-update-slice_fusion.5.refs_4_), channel_id=1, source_target_pairs={{0,32},{4,12},{8,40},{12,4},{16,48},{20,28},{24,56},{28,20},{32,0}... | collective-permute-start | bytes 2359304 | tf_op jit(solution)/shard_map/ppermute | solution.py:49
  30.5 21.1 %collective-permute-start.10 = (bf16[16,192,128]{2,1,0:T(8,128)(2,1)S(1)}, bf16[16,192,128]{2,1,0:T(8,128)(2,1)S(1)}, u32[]{:S(2)}, u32[]{:S(2)}) collective-permute-start(bf16[16,192,128]{2,1,0:T(8,128)(2,1)S(1)} %constant_dynamic-update-slice_fusion.refs_0_), channel_id=1, source_target_pairs={{0,4},{4,0},{8,12},{12,8},{16,20},{20,16},{24,28},{28,24},{32,36},... | collective-permute-start | bytes 2359304 | tf_op jit(solution)/shard_map/ppermute | solution.py:49
  33.5 18.1 %collective-permute-start.13 = (bf16[16,192,128]{2,1,0:T(8,128)(2,1)S(1)}, bf16[16,192,128]{2,1,0:T(8,128)(2,1)S(1)}, u32[]{:S(2)}, u32[]{:S(2)}) collective-permute-start(bf16[16,192,128]{2,1,0:T(8,128)(2,1)S(1)} %constant_dynamic-update-slice_fusion.5.refs_4_), channel_id=1, source_target_pairs={{0,4},{4,0},{8,12},{12,8},{16,20},{20,16},{24,28},{28,24},{32,36},... | collective-permute-start | bytes 2359304 | tf_op jit(solution)/shard_map/ppermute | solution.py:49
  40.8 10.8 %collective-permute-start.11 = (bf16[16,192,128]{2,1,0:T(8,128)(2,1)S(1)}, bf16[16,192,128]{2,1,0:T(8,128)(2,1)S(1)}, u32[]{:S(2)}, u32[]{:S(2)}) collective-permute-start(bf16[16,192,128]{2,1,0:T(8,128)(2,1)S(1)} %collective-permute-done.9.refs_1_), channel_id=1, source_target_pairs={{0,4},{4,0},{8,12},{12,8},{16,20},{20,16},{24,28},{28,24},{32,36},... | collective-permute-start | bytes 2359304 | tf_op jit(solution)/shard_map/ppermute | solution.py:49
  43.8 7.8 %collective-permute-start.14 = (bf16[16,192,128]{2,1,0:T(8,128)(2,1)S(1)}, bf16[16,192,128]{2,1,0:T(8,128)(2,1)S(1)}, u32[]{:S(2)}, u32[]{:S(2)}) collective-permute-start(bf16[16,192,128]{2,1,0:T(8,128)(2,1)S(1)} %collective-permute-done.12.refs_5_), channel_id=1, source_target_pairs={{0,4},{4,0},{8,12},{12,8},{16,20},{20,16},{24,28},{28,24},{32,36},... | collective-permute-start | bytes 2359304 | tf_op jit(solution)/shard_map/ppermute | solution.py:49
  45.3 11.0 %collective-permute-start.8 = (bf16[192,512]{1,0:T(8,128)(2,1)S(1)}, bf16[192,512]{1,0:T(8,128)(2,1)S(1)}, u32[]{:S(2)}, u32[]{:S(2)}) collective-permute-start(bf16[192,512]{1,0:T(8,128)(2,1)S(1)} %get-tuple-element.11), channel_id=1, source_target_pairs={{0,252},{4,248},{8,244},{12,240},{16,236},{20,232},{24,228},{28,22... | collective-permute-start | bytes 589832 | tf_op jit(solution)/shard_map/ppermute | solution.py:49
  51.6 48.0 %slice-start = ((s8[8388608]{0:T(1024)(128)(4,1)}), s8[4194304]{0:T(1024)(128)(4,1)S(1)}, s32[]{:S(2)}) async-start(s8[8388608]{0:T(1024)(128)(4,1)} %bitcast.10), calls=%async_computation | async-start | bytes 8388608
  55.4 44.2 %slice-start.1 = ((s8[8388608]{0:T(1024)(128)(4,1)}), s8[4194304]{0:T(1024)(128)(4,1)S(1)}, s32[]{:S(2)}) async-start(s8[8388608]{0:T(1024)(128)(4,1)} %bitcast.10), calls=%async_computation.1 | async-start | bytes 8388608
  74.9 13.6 %collective-permute-start.15 = (bf16[192,512]{1,0:T(8,128)(2,1)S(1)}, bf16[192,512]{1,0:T(8,128)(2,1)S(1)}, u32[]{:S(2)}, u32[]{:S(2)}) collective-permute-start(bf16[192,512]{1,0:T(8,128)(2,1)S(1)} %shard_map.65), channel_id=1, source_target_pairs={{0,252},{4,248},{8,244},{12,240},{16,236},{20,232},{24,228},{28,22... | collective-permute-start | bytes 589832 | tf_op jit(solution)/shard_map/ppermute | solution.py:49
  75.0 13.5 %collective-permute-start.18 = (bf16[192,512]{1,0:T(8,128)(2,1)S(1)}, bf16[192,512]{1,0:T(8,128)(2,1)S(1)}, u32[]{:S(2)}, u32[]{:S(2)}) collective-permute-start(bf16[192,512]{1,0:T(8,128)(2,1)S(1)} %shard_map.64.refs_0_), channel_id=1, source_target_pairs={{0,1},{1,0},{2,3},{3,2},{4,7},{5,6},{6,5},{7,4},{8,9},{9,8},{10,11... | collective-permute-start | bytes 589832 | tf_op jit(solution)/shard_map/ppermute | solution.py:53
  88.5 11.0 %collective-permute-start.16 = (bf16[192,512]{1,0:T(8,128)(2,1)S(1)}, bf16[192,512]{1,0:T(8,128)(2,1)S(1)}, u32[]{:S(2)}, u32[]{:S(2)}) collective-permute-start(bf16[192,512]{1,0:T(8,128)(2,1)S(1)} %collective-permute-done.15.refs_1_), channel_id=1, source_target_pairs={{0,1},{1,0},{2,3},{3,2},{4,7},{5,6},{6,5},{7,4},{8,9},{9,8},{10,11... | collective-permute-start | bytes 589832 | tf_op jit(solution)/shard_map/ppermute | solution.py:53
  88.5 13.7 %collective-permute-start.19 = (bf16[2,192,512]{2,1,0:T(8,128)(2,1)S(1)}, bf16[2,192,512]{2,1,0:T(8,128)(2,1)S(1)}, u32[]{:S(2)}, u32[]{:S(2)}) collective-permute-start(bf16[2,192,512]{2,1,0:T(8,128)(2,1)S(1)} %pad_maximum_fusion.3), channel_id=1, source_target_pairs={{0,3},{1,2},{2,1},{3,0},{4,5},{5,4},{6,7},{7,6},{8,11},{9,10},{10,... | collective-permute-start | bytes 1179656 | tf_op jit(solution)/shard_map/ppermute | solution.py:53
  99.5 12.3 %collective-permute-start.17 = (bf16[2,192,512]{2,1,0:T(8,128)(2,1)S(1)}, bf16[2,192,512]{2,1,0:T(8,128)(2,1)S(1)}, u32[]{:S(2)}, u32[]{:S(2)}) collective-permute-start(bf16[2,192,512]{2,1,0:T(8,128)(2,1)S(1)} %pad_maximum_fusion.2), channel_id=1, source_target_pairs={{0,3},{1,2},{2,1},{3,0},{4,5},{5,4},{6,7},{7,6},{8,11},{9,10},{10,... | collective-permute-start | bytes 1179656 | tf_op jit(solution)/shard_map/ppermute | solution.py:53
where the time goes:
time: 114 us; the launch traced here: 113 us
  waiting for transfers between devices  51.7 us (45%)
  starting transfers between devices  32.2 us (28%)
  Pallas kernels  25.2 us (22%)
  local copies, waits for them, and re-layouts  2.07 us (2%)
  other arithmetic  1.84 us (2%)
    ppermute x16, waiting for transfers between devices, swap(): return lax.ppermute(a, 'ctx', pairs)  31.5 us
    ppermute x16, starting transfers between devices, swap(): return lax.ppermute(a, 'ctx', pairs)  26.3 us
    pallas_call x2, Pallas kernels, attention(): pl.pallas_call(functools.partial(attention_kernel, mirrored), out_shape=o...  22.2 us
    ppermute x4, waiting for transfers between devices, head_swap(): return lax.ppermute(a, ('ctx', 'head'), HEAD_STEPS[step])  20.2 us
    ppermute x4, starting transfers between devices, head_swap(): return lax.ppermute(a, ('ctx', 'head'), HEAD_STEPS[step])  5.86 us
    pallas_call x3, Pallas kernels, project(): pl.pallas_call(functools.partial(project_kernel, sources), out_shape=jax....  2.99 us
  transfers between devices with their start and end apart: 20, of which 12 were waited for; matrix products, arithmetic and copies ran while one was open for 3% of the time, Pallas kernels for 5%

commit v1 on v0

--- a/solution.py
+++ b/solution.py
@@ -15,6 +15,7 @@
 TILES = SEQ // TILE
 HEADS = 32
 STRIP = 32
+UNROLL = 4
 GROUP = 4
 NEG = -1e30
 
@@ -102,9 +103,10 @@
         return lax.fori_loop(low, diag + 1, put, counts)
 
     masked, plain = lax.fori_loop(0, GROUP, list_unit, (0, 0))
-    odd = plain % 2
-    items[0, masked] = items[1, jnp.maximum(plain - 1, 0)]
-    masked, plain = masked + odd, plain - odd
+    left = plain % UNROLL
+    for n in range(UNROLL - 1):
+        items[0, masked + n] = items[1, jnp.maximum(plain - 1 - n, 0)]
+    masked, plain = masked + left, plain - left
     items[0, masked] = items[0, 0]
     items[0, masked + 1] = items[0, 0]
     items[1, plain] = 0
@@ -156,27 +158,27 @@
         pv = jnp.dot(p_ref[...], vbuf[span(item % TILES)], preferred_element_type=jnp.float32)
         acc[u] = acc[u] * f_ref[...] + pv
 
-    def run(kind, count, use_mask):
+    def run(kind, count, use_mask, unroll):
         pb[...] = jnp.zeros_like(pb)
         fb[...] = jnp.ones_like(fb)
         score(items[kind, 0], sa)
 
-        def two(k, before):
-            i = 2 * k
-            now, then, later = items[kind, i], items[kind, i + 1], items[kind, i + 2]
-            score(then, sb)
-            gather_values(before, pb, fb)
-            soften(now, sa, pa, fa, use_mask, True)
-            score(later, sa)
-            gather_values(now, pa, fa)
-            soften(then, sb, pb, fb, use_mask, i + 1 < count)
-            return then
-
-        before = lax.fori_loop(0, (count + 1) // 2, two, items[kind, 0])
+        def some(k, before):
+            i = unroll * k
+            for n in range(unroll):
+                here, there = ((sa, pa, fa), (sb, pb, fb))[:: 1 if n % 2 == 0 else -1]
+                now = items[kind, i + n]
+                score(items[kind, i + n + 1], there[0])
+                gather_values(before, there[1], there[2])
+                soften(now, *here, use_mask, True if n == 0 else i + n < count)
+                before = now
+            return before
+
+        before = lax.fori_loop(0, (count + unroll - 1) // unroll, some, items[kind, 0])
         gather_values(before, pb, fb)
 
-    run(0, masked, True)
-    run(1, plain, False)
+    run(0, masked, True, 2)
+    run(1, plain, False, UNROLL)
 
     for j in range(GROUP):
         total = jnp.sum(tot[j], axis=1, keepdims=True)

time: 114 us -> 113 us (level)
  the two profiles are of different devices: /device:TPU:1 before, /device:TPU:33 now
where the time goes in v1:
time: 113 us
  starting transfers between devices  50.6 us (45%)
  waiting for transfers between devices  33.7 us (30%)
  Pallas kernels  24.3 us (22%)
  local copies, waits for them, and re-layouts  2.07 us (2%)
  other arithmetic  1.84 us (2%)
    ppermute x16, starting transfers between devices, swap(): return lax.ppermute(a, 'ctx', pairs)  35.8 us
    pallas_call x2, Pallas kernels, attention(): pl.pallas_call(functools.partial(attention_kernel, mirrored), out_shape=o...  21.3 us
    ppermute x16, waiting for transfers between devices, swap(): return lax.ppermute(a, 'ctx', pairs)  17 us
    ppermute x4, waiting for transfers between devices, head_swap(): return lax.ppermute(a, ('ctx', 'head'), HEAD_STEPS[step])  16.7 us
    ppermute x4, starting transfers between devices, head_swap(): return lax.ppermute(a, ('ctx', 'head'), HEAD_STEPS[step])  14.8 us
    pallas_call x3, Pallas kernels, project(): pl.pallas_call(functools.partial(project_kernel, sources), out_shape=jax....  3.01 us
  transfers between devices with their start and end apart: 20, of which 11 were waited for; matrix products, arithmetic and copies ran while one was open for 3% of the time, Pallas kernels for 11%

profile of v1, /device:TPU:33, one launch (start us, length us, event | category | flops | bytes accessed | tf_op | source)
XLA Modules:
  0.0 112.8 jit_solution(1378655986644028978)
XLA Ops:
  4.3 2.8 %collective-permute-start.5 = (bf16[2,192,128]{2,1,0:T(8,128)(2,1)S(1)}, bf16[2,192,128]{2,1,0:T(8,128)(2,1)S(1)}, u32[]{:S(2)}, u32[]{:S(2)}) collective-permute-start(bf16[2,192,128]{2,1,0:T(8,128)(2,1)S(1)} %pad_maximum_fusion.7), channel_id=1, source_target_pairs={{0,24},{4,100},{8,16},{12,108},{16,8},{20,116},{24,0},{28,124},{32... | collective-permute-start | bytes 294920 | tf_op jit(solution)/shard_map/ppermute | solution.py:50
  7.3 1.9 %collective-permute-done.5 = bf16[2,192,128]{2,1,0:T(8,128)(2,1)S(1)} collective-permute-done((bf16[2,192,128]{2,1,0:T(8,128)(2,1)S(1)}, bf16[2,192,128]{2,1,0:T(8,128)(2,1)S(1)}, u32[]{:S(2)}, u32[]{:S(2)}) %collective-permute-start.5) | collective-permute-done | bytes 98336 | tf_op jit(solution)/shard_map/ppermute | solution.py:50
  9.3 1.4 %collective-permute-done.2 = bf16[2,192,128]{2,1,0:T(8,128)(2,1)S(1)} collective-permute-done((bf16[2,192,128]{2,1,0:T(8,128)(2,1)S(1)}, bf16[2,192,128]{2,1,0:T(8,128)(2,1)S(1)}, u32[]{:S(2)}, u32[]{:S(2)}) %collective-permute-start.2) | collective-permute-done | bytes 98336 | tf_op jit(solution)/shard_map/ppermute | solution.py:50
  12.1 2.0 %collective-permute-done.6 = bf16[4,192,128]{2,1,0:T(8,128)(2,1)S(1)} collective-permute-done((bf16[4,192,128]{2,1,0:T(8,128)(2,1)S(1)}, bf16[4,192,128]{2,1,0:T(8,128)(2,1)S(1)}, u32[]{:S(2)}, u32[]{:S(2)}) %collective-permute-start.6) | collective-permute-done | bytes 196640 | tf_op jit(solution)/shard_map/ppermute | solution.py:50
  14.1 2.3 %collective-permute-start.7 = (bf16[8,192,128]{2,1,0:T(8,128)(2,1)S(1)}, bf16[8,192,128]{2,1,0:T(8,128)(2,1)S(1)}, u32[]{:S(2)}, u32[]{:S(2)}) collective-permute-start(bf16[8,192,128]{2,1,0:T(8,128)(2,1)S(1)} %pad_maximum_fusion.1), channel_id=1, source_target_pairs={{0,96},{4,28},{8,104},{12,20},{16,112},{20,12},{24,120},{28,4},{32... | collective-permute-start | bytes 1179656 | tf_op jit(solution)/shard_map/ppermute | solution.py:50
  16.6 1.6 %collective-permute-start.4 = (bf16[8,192,128]{2,1,0:T(8,128)(2,1)S(1)}, bf16[8,192,128]{2,1,0:T(8,128)(2,1)S(1)}, u32[]{:S(2)}, u32[]{:S(2)}) collective-permute-start(bf16[8,192,128]{2,1,0:T(8,128)(2,1)S(1)} %pad_maximum_fusion), channel_id=1, source_target_pairs={{0,32},{4,12},{8,40},{12,4},{16,48},{20,28},{24,56},{28,20},{32,0}... | collective-permute-start | bytes 1179656 | tf_op jit(solution)/shard_map/ppermute | solution.py:50
  18.3 6.2 %collective-permute-done.7 = bf16[8,192,128]{2,1,0:T(8,128)(2,1)S(1)} collective-permute-done((bf16[8,192,128]{2,1,0:T(8,128)(2,1)S(1)}, bf16[8,192,128]{2,1,0:T(8,128)(2,1)S(1)}, u32[]{:S(2)}, u32[]{:S(2)}) %collective-permute-start.7) | collective-permute-done | bytes 393248 | tf_op jit(solution)/shard_map/ppermute | solution.py:50
  24.6 2.0 %collective-permute-start.9 = (bf16[16,192,128]{2,1,0:T(8,128)(2,1)S(1)}, bf16[16,192,128]{2,1,0:T(8,128)(2,1)S(1)}, u32[]{:S(2)}, u32[]{:S(2)}) collective-permute-start(bf16[16,192,128]{2,1,0:T(8,128)(2,1)S(1)} %constant_dynamic-update-slice_fusion.refs_0_), channel_id=1, source_target_pairs={{0,96},{4,28},{8,104},{12,20},{16,112},{20,12},{24,120},{28,4},{32... | collective-permute-start | bytes 2359304 | tf_op jit(solution)/shard_map/ppermute | solution.py:50
  26.6 8.9 %collective-permute-start.10 = (bf16[16,192,128]{2,1,0:T(8,128)(2,1)S(1)}, bf16[16,192,128]{2,1,0:T(8,128)(2,1)S(1)}, u32[]{:S(2)}, u32[]{:S(2)}) collective-permute-start(bf16[16,192,128]{2,1,0:T(8,128)(2,1)S(1)} %constant_dynamic-update-slice_fusion.refs_0_), channel_id=1, source_target_pairs={{0,4},{4,0},{8,12},{12,8},{16,20},{20,16},{24,28},{28,24},{32,36},... | collective-permute-start | bytes 2359304 | tf_op jit(solution)/shard_map/ppermute | solution.py:50
  35.4 1.6 %collective-permute-done.9.refs_1_ = bf16[16,192,128]{2,1,0:T(8,128)(2,1)S(1)} collective-permute-done((bf16[16,192,128]{2,1,0:T(8,128)(2,1)S(1)}, bf16[16,192,128]{2,1,0:T(8,128)(2,1)S(1)}, u32[]{:S(2)}, u32[]{:S(2)}) %collective-permute-start.9) | collective-permute-done | bytes 786464 | tf_op jit(solution)/shard_map/ppermute | solution.py:50
  37.0 8.6 %collective-permute-start.11 = (bf16[16,192,128]{2,1,0:T(8,128)(2,1)S(1)}, bf16[16,192,128]{2,1,0:T(8,128)(2,1)S(1)}, u32[]{:S(2)}, u32[]{:S(2)}) collective-permute-start(bf16[16,192,128]{2,1,0:T(8,128)(2,1)S(1)} %collective-permute-done.9.refs_1_), channel_id=1, source_target_pairs={{0,4},{4,0},{8,12},{12,8},{16,20},{20,16},{24,28},{28,24},{32,36},... | collective-permute-start | bytes 2359304 | tf_op jit(solution)/shard_map/ppermute | solution.py:50
  45.6 1.8 %collective-permute-start.14 = (bf16[16,192,128]{2,1,0:T(8,128)(2,1)S(1)}, bf16[16,192,128]{2,1,0:T(8,128)(2,1)S(1)}, u32[]{:S(2)}, u32[]{:S(2)}) collective-permute-start(bf16[16,192,128]{2,1,0:T(8,128)(2,1)S(1)} %collective-permute-done.12.refs_5_), channel_id=1, source_target_pairs={{0,4},{4,0},{8,12},{12,8},{16,20},{20,16},{24,28},{28,24},{32,36},... | collective-permute-start | bytes 2359304 | tf_op jit(solution)/shard_map/ppermute | solution.py:50
  47.5 1.8 %collective-permute-done.14.refs_7_ = bf16[16,192,128]{2,1,0:T(8,128)(2,1)S(1)} collective-permute-done((bf16[16,192,128]{2,1,0:T(8,128)(2,1)S(1)}, bf16[16,192,128]{2,1,0:T(8,128)(2,1)S(1)}, u32[]{:S(2)}, u32[]{:S(2)}) %collective-permute-start.14) | collective-permute-done | bytes 786464 | tf_op jit(solution)/shard_map/ppermute | solution.py:50
  49.3 11.1 %shard_map.64.refs_0_ = bf16[192,512]{1,0:T(8,128)(2,1)S(1)} custom-call(s32[96]{0:T(128)S(1)} %pad_add_fusion.table, bf16[192,512]{1,0:T(8,128)(2,1)S(1)} %get-tuple-element.15.q_ref, bf16[16,192,128]{2,1,0:T(8,128)(2,1)S(1)} %constant_dynamic-update-slice_fusion.refs_0_, bf16[16,192,128]{2,1,0:T(8,128)(2,1)S(1)} %collective-permute-done.9.refs_1_, ...), custom_call_target="tpu_custom_call" | custom-call | flops 4000000000 | bytes 8000000 | tf_op jit(solution)/shard_map/pallas_call | solution.py:192
  60.4 10.2 %shard_map.65 = bf16[192,512]{1,0:T(8,128)(2,1)S(1)} custom-call(s32[96]{0:T(128)S(1)} %pad_add_fusion.table, bf16[192,512]{1,0:T(8,128)(2,1)S(1)} %collective-permute-done.8.q_ref, bf16[16,192,128]{2,1,0:T(8,128)(2,1)S(1)} %constant_dynamic-update-slice_fusion.refs_0_, bf16[16,192,128]{2,1,0:T(8,128)(2,1)S(1)} %collective-permute-done.9.refs_1_, ...), custom_call_target="tpu_custom_call" | custom-call | flops 4000000000 | bytes 8000000 | tf_op jit(solution)/shard_map/pallas_call | solution.py:192
  70.7 5.6 %collective-permute-start.15 = (bf16[192,512]{1,0:T(8,128)(2,1)S(1)}, bf16[192,512]{1,0:T(8,128)(2,1)S(1)}, u32[]{:S(2)}, u32[]{:S(2)}) collective-permute-start(bf16[192,512]{1,0:T(8,128)(2,1)S(1)} %shard_map.65), channel_id=1, source_target_pairs={{0,252},{4,248},{8,244},{12,240},{16,236},{20,232},{24,228},{28,22... | collective-permute-start | bytes 589832 | tf_op jit(solution)/shard_map/ppermute | solution.py:50
  76.2 3.6 %collective-permute-start.18 = (bf16[192,512]{1,0:T(8,128)(2,1)S(1)}, bf16[192,512]{1,0:T(8,128)(2,1)S(1)}, u32[]{:S(2)}, u32[]{:S(2)}) collective-permute-start(bf16[192,512]{1,0:T(8,128)(2,1)S(1)} %shard_map.64.refs_0_), channel_id=1, source_target_pairs={{0,1},{1,0},{2,3},{3,2},{4,7},{5,6},{6,5},{7,4},{8,9},{9,8},{10,11... | collective-permute-start | bytes 589832 | tf_op jit(solution)/shard_map/ppermute | solution.py:54
  79.8 1.9 %collective-permute-done.15.refs_1_ = bf16[192,512]{1,0:T(8,128)(2,1)S(1)} collective-permute-done((bf16[192,512]{1,0:T(8,128)(2,1)S(1)}, bf16[192,512]{1,0:T(8,128)(2,1)S(1)}, u32[]{:S(2)}, u32[]{:S(2)}) %collective-permute-start.15) | collective-permute-done | bytes 196640 | tf_op jit(solution)/shard_map/ppermute | solution.py:50
  81.7 7.2 %collective-permute-start.16 = (bf16[192,512]{1,0:T(8,128)(2,1)S(1)}, bf16[192,512]{1,0:T(8,128)(2,1)S(1)}, u32[]{:S(2)}, u32[]{:S(2)}) collective-permute-start(bf16[192,512]{1,0:T(8,128)(2,1)S(1)} %collective-permute-done.15.refs_1_), channel_id=1, source_target_pairs={{0,1},{1,0},{2,3},{3,2},{4,7},{5,6},{6,5},{7,4},{8,9},{9,8},{10,11... | collective-permute-start | bytes 589832 | tf_op jit(solution)/shard_map/ppermute | solution.py:54
  88.9 1.5 %collective-permute-start.19 = (bf16[2,192,512]{2,1,0:T(8,128)(2,1)S(1)}, bf16[2,192,512]{2,1,0:T(8,128)(2,1)S(1)}, u32[]{:S(2)}, u32[]{:S(2)}) collective-permute-start(bf16[2,192,512]{2,1,0:T(8,128)(2,1)S(1)} %pad_maximum_fusion.3), channel_id=1, source_target_pairs={{0,3},{1,2},{2,1},{3,0},{4,5},{5,4},{6,7},{7,6},{8,11},{9,10},{10,... | collective-permute-start | bytes 1179656 | tf_op jit(solution)/shard_map/ppermute | solution.py:54
  90.4 9.3 %collective-permute-done.16.refs_0_ = bf16[192,512]{1,0:T(8,128)(2,1)S(1)} collective-permute-done((bf16[192,512]{1,0:T(8,128)(2,1)S(1)}, bf16[192,512]{1,0:T(8,128)(2,1)S(1)}, u32[]{:S(2)}, u32[]{:S(2)}) %collective-permute-start.16) | collective-permute-done | bytes 196640 | tf_op jit(solution)/shard_map/ppermute | solution.py:54
  99.8 2.5 %collective-permute-start.17 = (bf16[2,192,512]{2,1,0:T(8,128)(2,1)S(1)}, bf16[2,192,512]{2,1,0:T(8,128)(2,1)S(1)}, u32[]{:S(2)}, u32[]{:S(2)}) collective-permute-start(bf16[2,192,512]{2,1,0:T(8,128)(2,1)S(1)} %pad_maximum_fusion.2), channel_id=1, source_target_pairs={{0,3},{1,2},{2,1},{3,0},{4,5},{5,4},{6,7},{7,6},{8,11},{9,10},{10,... | collective-permute-start | bytes 1179656 | tf_op jit(solution)/shard_map/ppermute | solution.py:54
  103.7 7.4 %collective-permute-done.17.refs_1_ = bf16[2,192,512]{2,1,0:T(8,128)(2,1)S(1)} collective-permute-done((bf16[2,192,512]{2,1,0:T(8,128)(2,1)S(1)}, bf16[2,192,512]{2,1,0:T(8,128)(2,1)S(1)}, u32[]{:S(2)}, u32[]{:S(2)}) %collective-permute-start.17) | collective-permute-done | bytes 393248 | tf_op jit(solution)/shard_map/ppermute | solution.py:54
  111.2 1.6 %shard_map.68 = bf16[192,1024]{1,0:T(8,128)(2,1)} custom-call(bf16[192,512]{1,0:T(8,128)(2,1)S(1)} %collective-permute-done.16.refs_0_, bf16[2,192,512]{2,1,0:T(8,128)(2,1)S(1)} %collective-permute-done.17.refs_1_, bf16[4096,1024]{1,0:T(8,128)(2,1)S(1)} %bitcast.11, f32[192,1024]{1,0:T(8,128)S(1)} %shard_map.67.refs_3_), custom_call_target="tpu_custom_call" | custom-call | flops 600000000 | bytes 6000000 | tf_op jit(solution)/shard_map/pallas_call | solution.py:239
  (46 shorter events, 7.9 us)
Async XLA Ops:
  0.9 3.4 %collective-permute-start.1 = (bf16[2,192,128]{2,1,0:T(8,128)(2,1)S(1)}, bf16[2,192,128]{2,1,0:T(8,128)(2,1)S(1)}, u32[]{:S(2)}, u32[]{:S(2)}) collective-permute-start(bf16[2,192,128]{2,1,0:T(8,128)(2,1)S(1)} %get-tuple-element.17), channel_id=1, source_target_pairs={{0,128},{4,0},{8,136},{12,8},{16,144},{20,16},{24,152},{28,24},{32... | collective-permute-start | bytes 294920 | tf_op jit(solution)/shard_map/ppermute | solution.py:50
  1.0 3.2 %collective-permute-start = (bf16[2,192,128]{2,1,0:T(8,128)(2,1)S(1)}, bf16[2,192,128]{2,1,0:T(8,128)(2,1)S(1)}, u32[]{:S(2)}, u32[]{:S(2)}) collective-permute-start(bf16[2,192,128]{2,1,0:T(8,128)(2,1)S(1)} %get-tuple-element.18), channel_id=1, source_target_pairs={{0,0},{4,128},{8,8},{12,136},{16,16},{20,144},{24,24},{28,152},{32... | collective-permute-start | bytes 294920 | tf_op jit(solution)/shard_map/ppermute | solution.py:50
  4.3 4.8 %collective-permute-start.5 = (bf16[2,192,128]{2,1,0:T(8,128)(2,1)S(1)}, bf16[2,192,128]{2,1,0:T(8,128)(2,1)S(1)}, u32[]{:S(2)}, u32[]{:S(2)}) collective-permute-start(bf16[2,192,128]{2,1,0:T(8,128)(2,1)S(1)} %pad_maximum_fusion.7), channel_id=1, source_target_pairs={{0,24},{4,100},{8,16},{12,108},{16,8},{20,116},{24,0},{28,124},{32... | collective-permute-start | bytes 294920 | tf_op jit(solution)/shard_map/ppermute | solution.py:50
  7.2 3.6 %collective-permute-start.2 = (bf16[2,192,128]{2,1,0:T(8,128)(2,1)S(1)}, bf16[2,192,128]{2,1,0:T(8,128)(2,1)S(1)}, u32[]{:S(2)}, u32[]{:S(2)}) collective-permute-start(bf16[2,192,128]{2,1,0:T(8,128)(2,1)S(1)} %pad_maximum_fusion.6), channel_id=1, source_target_pairs={{0,8},{4,36},{8,0},{12,44},{16,24},{20,52},{24,16},{28,60},{32,40}... | collective-permute-start | bytes 294920 | tf_op jit(solution)/shard_map/ppermute | solution.py:50
  9.2 4.9 %collective-permute-start.6 = (bf16[4,192,128]{2,1,0:T(8,128)(2,1)S(1)}, bf16[4,192,128]{2,1,0:T(8,128)(2,1)S(1)}, u32[]{:S(2)}, u32[]{:S(2)}) collective-permute-start(bf16[4,192,128]{2,1,0:T(8,128)(2,1)S(1)} %pad_maximum_fusion.5), channel_id=1, source_target_pairs={{0,8},{4,36},{8,0},{12,44},{16,24},{20,52},{24,16},{28,60},{32,40}... | collective-permute-start | bytes 589832 | tf_op jit(solution)/shard_map/ppermute | solution.py:50
  10.8 5.8 %collective-permute-start.3 = (bf16[4,192,128]{2,1,0:T(8,128)(2,1)S(1)}, bf16[4,192,128]{2,1,0:T(8,128)(2,1)S(1)}, u32[]{:S(2)}, u32[]{:S(2)}) collective-permute-start(bf16[4,192,128]{2,1,0:T(8,128)(2,1)S(1)} %pad_maximum_fusion.4), channel_id=1, source_target_pairs={{0,24},{4,100},{8,16},{12,108},{16,8},{20,116},{24,0},{28,124},{32... | collective-permute-start | bytes 589832 | tf_op jit(solution)/shard_map/ppermute | solution.py:50
  14.1 10.3 %collective-permute-start.7 = (bf16[8,192,128]{2,1,0:T(8,128)(2,1)S(1)}, bf16[8,192,128]{2,1,0:T(8,128)(2,1)S(1)}, u32[]{:S(2)}, u32[]{:S(2)}) collective-permute-start(bf16[8,192,128]{2,1,0:T(8,128)(2,1)S(1)} %pad_maximum_fusion.1), channel_id=1, source_target_pairs={{0,96},{4,28},{8,104},{12,20},{16,112},{20,12},{24,120},{28,4},{32... | collective-permute-start | bytes 1179656 | tf_op jit(solution)/shard_map/ppermute | solution.py:50
  16.6 7.9 %collective-permute-start.4 = (bf16[8,192,128]{2,1,0:T(8,128)(2,1)S(1)}, bf16[8,192,128]{2,1,0:T(8,128)(2,1)S(1)}, u32[]{:S(2)}, u32[]{:S(2)}) collective-permute-start(bf16[8,192,128]{2,1,0:T(8,128)(2,1)S(1)} %pad_maximum_fusion), channel_id=1, source_target_pairs={{0,32},{4,12},{8,40},{12,4},{16,48},{20,28},{24,56},{28,20},{32,0}... | collective-permute-start | bytes 1179656 | tf_op jit(solution)/shard_map/ppermute | solution.py:50
  24.6 12.4 %collective-permute-start.9 = (bf16[16,192,128]{2,1,0:T(8,128)(2,1)S(1)}, bf16[16,192,128]{2,1,0:T(8,128)(2,1)S(1)}, u32[]{:S(2)}, u32[]{:S(2)}) collective-permute-start(bf16[16,192,128]{2,1,0:T(8,128)(2,1)S(1)} %constant_dynamic-update-slice_fusion.refs_0_), channel_id=1, source_target_pairs={{0,96},{4,28},{8,104},{12,20},{16,112},{20,12},{24,120},{28,4},{32... | collective-permute-start | bytes 2359304 | tf_op jit(solution)/shard_map/ppermute | solution.py:50
  26.6 19.1 %collective-permute-start.12 = (bf16[16,192,128]{2,1,0:T(8,128)(2,1)S(1)}, bf16[16,192,128]{2,1,0:T(8,128)(2,1)S(1)}, u32[]{:S(2)}, u32[]{:S(2)}) collective-permute-start(bf16[16,192,128]{2,1,0:T(8,128)(2,1)S(1)} %constant_dynamic-update-slice_fusion.5.refs_4_), channel_id=1, source_target_pairs={{0,32},{4,12},{8,40},{12,4},{16,48},{20,28},{24,56},{28,20},{32,0}... | collective-permute-start | bytes 2359304 | tf_op jit(solution)/shard_map/ppermute | solution.py:50
  26.6 20.9 %collective-permute-start.10 = (bf16[16,192,128]{2,1,0:T(8,128)(2,1)S(1)}, bf16[16,192,128]{2,1,0:T(8,128)(2,1)S(1)}, u32[]{:S(2)}, u32[]{:S(2)}) collective-permute-start(bf16[16,192,128]{2,1,0:T(8,128)(2,1)S(1)} %constant_dynamic-update-slice_fusion.refs_0_), channel_id=1, source_target_pairs={{0,4},{4,0},{8,12},{12,8},{16,20},{20,16},{24,28},{28,24},{32,36},... | collective-permute-start | bytes 2359304 | tf_op jit(solution)/shard_map/ppermute | solution.py:50
  35.4 12.0 %collective-permute-start.13 = (bf16[16,192,128]{2,1,0:T(8,128)(2,1)S(1)}, bf16[16,192,128]{2,1,0:T(8,128)(2,1)S(1)}, u32[]{:S(2)}, u32[]{:S(2)}) collective-permute-start(bf16[16,192,128]{2,1,0:T(8,128)(2,1)S(1)} %constant_dynamic-update-slice_fusion.5.refs_4_), channel_id=1, source_target_pairs={{0,4},{4,0},{8,12},{12,8},{16,20},{20,16},{24,28},{28,24},{32,36},... | collective-permute-start | bytes 2359304 | tf_op jit(solution)/shard_map/ppermute | solution.py:50
  37.0 10.5 %collective-permute-start.11 = (bf16[16,192,128]{2,1,0:T(8,128)(2,1)S(1)}, bf16[16,192,128]{2,1,0:T(8,128)(2,1)S(1)}, u32[]{:S(2)}, u32[]{:S(2)}) collective-permute-start(bf16[16,192,128]{2,1,0:T(8,128)(2,1)S(1)} %collective-permute-done.9.refs_1_), channel_id=1, source_target_pairs={{0,4},{4,0},{8,12},{12,8},{16,20},{20,16},{24,28},{28,24},{32,36},... | collective-permute-start | bytes 2359304 | tf_op jit(solution)/shard_map/ppermute | solution.py:50
  45.6 3.7 %collective-permute-start.14 = (bf16[16,192,128]{2,1,0:T(8,128)(2,1)S(1)}, bf16[16,192,128]{2,1,0:T(8,128)(2,1)S(1)}, u32[]{:S(2)}, u32[]{:S(2)}) collective-permute-start(bf16[16,192,128]{2,1,0:T(8,128)(2,1)S(1)} %collective-permute-done.12.refs_5_), channel_id=1, source_target_pairs={{0,4},{4,0},{8,12},{12,8},{16,20},{20,16},{24,28},{28,24},{32,36},... | collective-permute-start | bytes 2359304 | tf_op jit(solution)/shard_map/ppermute | solution.py:50
  47.4 13.0 %collective-permute-start.8 = (bf16[192,512]{1,0:T(8,128)(2,1)S(1)}, bf16[192,512]{1,0:T(8,128)(2,1)S(1)}, u32[]{:S(2)}, u32[]{:S(2)}) collective-permute-start(bf16[192,512]{1,0:T(8,128)(2,1)S(1)} %get-tuple-element.11), channel_id=1, source_target_pairs={{0,252},{4,248},{8,244},{12,240},{16,236},{20,232},{24,228},{28,22... | collective-permute-start | bytes 589832 | tf_op jit(solution)/shard_map/ppermute | solution.py:50
  49.3 53.0 %slice-start = ((s8[8388608]{0:T(1024)(128)(4,1)}), s8[4194304]{0:T(1024)(128)(4,1)S(1)}, s32[]{:S(2)}) async-start(s8[8388608]{0:T(1024)(128)(4,1)} %bitcast.10), calls=%async_computation | async-start | bytes 8388608
  60.4 41.9 %slice-start.1 = ((s8[8388608]{0:T(1024)(128)(4,1)}), s8[4194304]{0:T(1024)(128)(4,1)S(1)}, s32[]{:S(2)}) async-start(s8[8388608]{0:T(1024)(128)(4,1)} %bitcast.10), calls=%async_computation.1 | async-start | bytes 8388608
  70.7 11.1 %collective-permute-start.15 = (bf16[192,512]{1,0:T(8,128)(2,1)S(1)}, bf16[192,512]{1,0:T(8,128)(2,1)S(1)}, u32[]{:S(2)}, u32[]{:S(2)}) collective-permute-start(bf16[192,512]{1,0:T(8,128)(2,1)S(1)} %shard_map.65), channel_id=1, source_target_pairs={{0,252},{4,248},{8,244},{12,240},{16,236},{20,232},{24,228},{28,22... | collective-permute-start | bytes 589832 | tf_op jit(solution)/shard_map/ppermute | solution.py:50
  76.2 12.7 %collective-permute-start.18 = (bf16[192,512]{1,0:T(8,128)(2,1)S(1)}, bf16[192,512]{1,0:T(8,128)(2,1)S(1)}, u32[]{:S(2)}, u32[]{:S(2)}) collective-permute-start(bf16[192,512]{1,0:T(8,128)(2,1)S(1)} %shard_map.64.refs_0_), channel_id=1, source_target_pairs={{0,1},{1,0},{2,3},{3,2},{4,7},{5,6},{6,5},{7,4},{8,9},{9,8},{10,11... | collective-permute-start | bytes 589832 | tf_op jit(solution)/shard_map/ppermute | solution.py:54
  81.7 18.0 %collective-permute-start.16 = (bf16[192,512]{1,0:T(8,128)(2,1)S(1)}, bf16[192,512]{1,0:T(8,128)(2,1)S(1)}, u32[]{:S(2)}, u32[]{:S(2)}) collective-permute-start(bf16[192,512]{1,0:T(8,128)(2,1)S(1)} %collective-permute-done.15.refs_1_), channel_id=1, source_target_pairs={{0,1},{1,0},{2,3},{3,2},{4,7},{5,6},{6,5},{7,4},{8,9},{9,8},{10,11... | collective-permute-start | bytes 589832 | tf_op jit(solution)/shard_map/ppermute | solution.py:54
  88.9 13.9 %collective-permute-start.19 = (bf16[2,192,512]{2,1,0:T(8,128)(2,1)S(1)}, bf16[2,192,512]{2,1,0:T(8,128)(2,1)S(1)}, u32[]{:S(2)}, u32[]{:S(2)}) collective-permute-start(bf16[2,192,512]{2,1,0:T(8,128)(2,1)S(1)} %pad_maximum_fusion.3), channel_id=1, source_target_pairs={{0,3},{1,2},{2,1},{3,0},{4,5},{5,4},{6,7},{7,6},{8,11},{9,10},{10,... | collective-permute-start | bytes 1179656 | tf_op jit(solution)/shard_map/ppermute | solution.py:54
  99.8 11.4 %collective-permute-start.17 = (bf16[2,192,512]{2,1,0:T(8,128)(2,1)S(1)}, bf16[2,192,512]{2,1,0:T(8,128)(2,1)S(1)}, u32[]{:S(2)}, u32[]{:S(2)}) collective-permute-start(bf16[2,192,512]{2,1,0:T(8,128)(2,1)S(1)} %pad_maximum_fusion.2), channel_id=1, source_target_pairs={{0,3},{1,2},{2,1},{3,0},{4,5},{5,4},{6,7},{7,6},{8,11},{9,10},{10,... | collective-permute-start | bytes 1179656 | tf_op jit(solution)/shard_map/ppermute | solution.py:54

commit v2 on v1

--- a/solution.py
+++ b/solution.py
@@ -168,8 +168,8 @@
             for n in range(unroll):
                 here, there = ((sa, pa, fa), (sb, pb, fb))[:: 1 if n % 2 == 0 else -1]
                 now = items[kind, i + n]
+                gather_values(before, there[1], there[2])
                 score(items[kind, i + n + 1], there[0])
-                gather_values(before, there[1], there[2])
                 soften(now, *here, use_mask, True if n == 0 else i + n < count)
                 before = now
             return before
@@ -281,10 +281,14 @@
     total = project(((0, SAME), (0, NEAR)), jnp.float32, (mine, mine_near), out_weight)
     their_near = head_swap(theirs, 0)
     their_far = head_swap(jnp.stack([theirs, their_near]), 1)
-    total = project(((0, FAR), (1, SAME)), jnp.float32, (mine_far, theirs), out_weight, total)
-    return project(
-        ((1, NEAR), (1, FAR)), jnp.bfloat16, (their_near, their_far), out_weight, total
+    total = project(
+        ((0, FAR), (1, SAME), (1, NEAR)),
+        jnp.float32,
+        (mine_far, theirs, their_near),
+        out_weight,
+        total,
     )
+    return project(((1, FAR),), jnp.bfloat16, (their_far,), out_weight, total)
 
 
 def solution(mesh):

time: 113 us -> 113 us (level)
  the two profiles are of different devices: /device:TPU:33 before, /device:TPU:0 now
where the time goes in v2:
time: 113 us
  waiting for transfers between devices  61.4 us (54%)
  Pallas kernels  24.3 us (22%)
  starting transfers between devices  22.8 us (20%)
  local copies, waits for them, and re-layouts  2.07 us (2%)
  other arithmetic  1.84 us (2%)
    ppermute x16, waiting for transfers between devices, swap(): return lax.ppermute(a, 'ctx', pairs)  38.4 us
    ppermute x4, waiting for transfers between devices, head_swap(): return lax.ppermute(a, ('ctx', 'head'), HEAD_STEPS[step])  22.9 us
    pallas_call x2, Pallas kernels, attention(): pl.pallas_call(functools.partial(attention_kernel, mirrored), out_shape=o...  21.3 us
    ppermute x16, starting transfers between devices, swap(): return lax.ppermute(a, 'ctx', pairs)  20.1 us
    pallas_call x3, Pallas kernels, project(): pl.pallas_call(functools.partial(project_kernel, sources), out_shape=jax....  3 us
    ppermute x4, starting transfers between devices, head_swap(): return lax.ppermute(a, ('ctx', 'head'), HEAD_STEPS[step])  2.73 us
  transfers between devices with their start and end apart: 20, of which 12 were waited for; matrix products, arithmetic and copies ran while one was open for 3% of the time, Pallas kernels for 5%

profile of v2, /device:TPU:0, one launch (start us, length us, event | category | flops | bytes accessed | tf_op | source)
XLA Modules:
  0.0 112.7 jit_solution(7709178782677076111)
XLA Ops:
  2.6 1.0 constant_dynamic-slice_fusion
  4.5 2.8 %collective-permute-start.5 = (bf16[2,192,128]{2,1,0:T(8,128)(2,1)S(1)}, bf16[2,192,128]{2,1,0:T(8,128)(2,1)S(1)}, u32[]{:S(2)}, u32[]{:S(2)}) collective-permute-start(bf16[2,192,128]{2,1,0:T(8,128)(2,1)S(1)} %pad_maximum_fusion.7), channel_id=1, source_target_pairs={{0,24},{4,100},{8,16},{12,108},{16,8},{20,116},{24,0},{28,124},{32... | collective-permute-start | bytes 294920 | tf_op jit(solution)/shard_map/ppermute | solution.py:50
  7.7 2.7 %collective-permute-done.5 = bf16[2,192,128]{2,1,0:T(8,128)(2,1)S(1)} collective-permute-done((bf16[2,192,128]{2,1,0:T(8,128)(2,1)S(1)}, bf16[2,192,128]{2,1,0:T(8,128)(2,1)S(1)}, u32[]{:S(2)}, u32[]{:S(2)}) %collective-permute-start.5) | collective-permute-done | bytes 98336 | tf_op jit(solution)/shard_map/ppermute | solution.py:50
  10.8 1.3 %collective-permute-done.2 = bf16[2,192,128]{2,1,0:T(8,128)(2,1)S(1)} collective-permute-done((bf16[2,192,128]{2,1,0:T(8,128)(2,1)S(1)}, bf16[2,192,128]{2,1,0:T(8,128)(2,1)S(1)}, u32[]{:S(2)}, u32[]{:S(2)}) %collective-permute-start.2) | collective-permute-done | bytes 98336 | tf_op jit(solution)/shard_map/ppermute | solution.py:50
  12.1 1.3 %collective-permute-start.3 = (bf16[4,192,128]{2,1,0:T(8,128)(2,1)S(1)}, bf16[4,192,128]{2,1,0:T(8,128)(2,1)S(1)}, u32[]{:S(2)}, u32[]{:S(2)}) collective-permute-start(bf16[4,192,128]{2,1,0:T(8,128)(2,1)S(1)} %pad_maximum_fusion.4), channel_id=1, source_target_pairs={{0,24},{4,100},{8,16},{12,108},{16,8},{20,116},{24,0},{28,124},{32... | collective-permute-start | bytes 589832 | tf_op jit(solution)/shard_map/ppermute | solution.py:50
  13.5 2.8 %collective-permute-done.6 = bf16[4,192,128]{2,1,0:T(8,128)(2,1)S(1)} collective-permute-done((bf16[4,192,128]{2,1,0:T(8,128)(2,1)S(1)}, bf16[4,192,128]{2,1,0:T(8,128)(2,1)S(1)}, u32[]{:S(2)}, u32[]{:S(2)}) %collective-permute-start.6) | collective-permute-done | bytes 196640 | tf_op jit(solution)/shard_map/ppermute | solution.py:50
  16.3 3.1 %collective-permute-start.7 = (bf16[8,192,128]{2,1,0:T(8,128)(2,1)S(1)}, bf16[8,192,128]{2,1,0:T(8,128)(2,1)S(1)}, u32[]{:S(2)}, u32[]{:S(2)}) collective-permute-start(bf16[8,192,128]{2,1,0:T(8,128)(2,1)S(1)} %pad_maximum_fusion.1), channel_id=1, source_target_pairs={{0,96},{4,28},{8,104},{12,20},{16,112},{20,12},{24,120},{28,4},{32... | collective-permute-start | bytes 1179656 | tf_op jit(solution)/shard_map/ppermute | solution.py:50
  19.4 1.4 %collective-permute-start.4 = (bf16[8,192,128]{2,1,0:T(8,128)(2,1)S(1)}, bf16[8,192,128]{2,1,0:T(8,128)(2,1)S(1)}, u32[]{:S(2)}, u32[]{:S(2)}) collective-permute-start(bf16[8,192,128]{2,1,0:T(8,128)(2,1)S(1)} %pad_maximum_fusion), channel_id=1, source_target_pairs={{0,32},{4,12},{8,40},{12,4},{16,48},{20,28},{24,56},{28,20},{32,0}... | collective-permute-start | bytes 1179656 | tf_op jit(solution)/shard_map/ppermute | solution.py:50
  20.9 4.5 %collective-permute-done.7 = bf16[8,192,128]{2,1,0:T(8,128)(2,1)S(1)} collective-permute-done((bf16[8,192,128]{2,1,0:T(8,128)(2,1)S(1)}, bf16[8,192,128]{2,1,0:T(8,128)(2,1)S(1)}, u32[]{:S(2)}, u32[]{:S(2)}) %collective-permute-start.7) | collective-permute-done | bytes 393248 | tf_op jit(solution)/shard_map/ppermute | solution.py:50
  25.4 1.9 %collective-permute-done.4 = bf16[8,192,128]{2,1,0:T(8,128)(2,1)S(1)} collective-permute-done((bf16[8,192,128]{2,1,0:T(8,128)(2,1)S(1)}, bf16[8,192,128]{2,1,0:T(8,128)(2,1)S(1)}, u32[]{:S(2)}, u32[]{:S(2)}) %collective-permute-start.4) | collective-permute-done | bytes 393248 | tf_op jit(solution)/shard_map/ppermute | solution.py:50
  27.3 2.8 %collective-permute-start.9 = (bf16[16,192,128]{2,1,0:T(8,128)(2,1)S(1)}, bf16[16,192,128]{2,1,0:T(8,128)(2,1)S(1)}, u32[]{:S(2)}, u32[]{:S(2)}) collective-permute-start(bf16[16,192,128]{2,1,0:T(8,128)(2,1)S(1)} %constant_dynamic-update-slice_fusion.refs_0_), channel_id=1, source_target_pairs={{0,96},{4,28},{8,104},{12,20},{16,112},{20,12},{24,120},{28,4},{32... | collective-permute-start | bytes 2359304 | tf_op jit(solution)/shard_map/ppermute | solution.py:50
  30.8 9.8 %collective-permute-done.9.refs_1_ = bf16[16,192,128]{2,1,0:T(8,128)(2,1)S(1)} collective-permute-done((bf16[16,192,128]{2,1,0:T(8,128)(2,1)S(1)}, bf16[16,192,128]{2,1,0:T(8,128)(2,1)S(1)}, u32[]{:S(2)}, u32[]{:S(2)}) %collective-permute-start.9) | collective-permute-done | bytes 786464 | tf_op jit(solution)/shard_map/ppermute | solution.py:50
  40.6 1.5 %collective-permute-done.12.refs_5_ = bf16[16,192,128]{2,1,0:T(8,128)(2,1)S(1)} collective-permute-done((bf16[16,192,128]{2,1,0:T(8,128)(2,1)S(1)}, bf16[16,192,128]{2,1,0:T(8,128)(2,1)S(1)}, u32[]{:S(2)}, u32[]{:S(2)}) %collective-permute-start.12) | collective-permute-done | bytes 786464 | tf_op jit(solution)/shard_map/ppermute | solution.py:50
  42.1 6.3 %collective-permute-start.8 = (bf16[192,512]{1,0:T(8,128)(2,1)S(1)}, bf16[192,512]{1,0:T(8,128)(2,1)S(1)}, u32[]{:S(2)}, u32[]{:S(2)}) collective-permute-start(bf16[192,512]{1,0:T(8,128)(2,1)S(1)} %get-tuple-element.11), channel_id=1, source_target_pairs={{0,252},{4,248},{8,244},{12,240},{16,236},{20,232},{24,228},{28,22... | collective-permute-start | bytes 589832 | tf_op jit(solution)/shard_map/ppermute | solution.py:50
  48.4 3.7 %shard_map.64.refs_0_ = bf16[192,512]{1,0:T(8,128)(2,1)S(1)} custom-call(s32[96]{0:T(128)S(1)} %pad_add_fusion.table, bf16[192,512]{1,0:T(8,128)(2,1)S(1)} %get-tuple-element.15.q_ref, bf16[16,192,128]{2,1,0:T(8,128)(2,1)S(1)} %constant_dynamic-update-slice_fusion.refs_0_, bf16[16,192,128]{2,1,0:T(8,128)(2,1)S(1)} %collective-permute-done.9.refs_1_, ...), custom_call_target="tpu_custom_call" | custom-call | flops 4000000000 | bytes 8000000 | tf_op jit(solution)/shard_map/pallas_call | solution.py:192
  52.2 1.3 %collective-permute-done.8.q_ref = bf16[192,512]{1,0:T(8,128)(2,1)S(1)} collective-permute-done((bf16[192,512]{1,0:T(8,128)(2,1)S(1)}, bf16[192,512]{1,0:T(8,128)(2,1)S(1)}, u32[]{:S(2)}, u32[]{:S(2)}) %collective-permute-start.8) | collective-permute-done | bytes 196640 | tf_op jit(solution)/shard_map/ppermute | solution.py:50
  53.5 17.6 %shard_map.65 = bf16[192,512]{1,0:T(8,128)(2,1)S(1)} custom-call(s32[96]{0:T(128)S(1)} %pad_add_fusion.table, bf16[192,512]{1,0:T(8,128)(2,1)S(1)} %collective-permute-done.8.q_ref, bf16[16,192,128]{2,1,0:T(8,128)(2,1)S(1)} %constant_dynamic-update-slice_fusion.refs_0_, bf16[16,192,128]{2,1,0:T(8,128)(2,1)S(1)} %collective-permute-done.9.refs_1_, ...), custom_call_target="tpu_custom_call" | custom-call | flops 4000000000 | bytes 8000000 | tf_op jit(solution)/shard_map/pallas_call | solution.py:192
  71.7 12.6 %collective-permute-done.15.refs_1_ = bf16[192,512]{1,0:T(8,128)(2,1)S(1)} collective-permute-done((bf16[192,512]{1,0:T(8,128)(2,1)S(1)}, bf16[192,512]{1,0:T(8,128)(2,1)S(1)}, u32[]{:S(2)}, u32[]{:S(2)}) %collective-permute-start.15) | collective-permute-done | bytes 196640 | tf_op jit(solution)/shard_map/ppermute | solution.py:50
  84.4 2.1 %collective-permute-start.19 = (bf16[2,192,512]{2,1,0:T(8,128)(2,1)S(1)}, bf16[2,192,512]{2,1,0:T(8,128)(2,1)S(1)}, u32[]{:S(2)}, u32[]{:S(2)}) collective-permute-start(bf16[2,192,512]{2,1,0:T(8,128)(2,1)S(1)} %pad_maximum_fusion.3), channel_id=1, source_target_pairs={{0,3},{1,2},{2,1},{3,0},{4,5},{5,4},{6,7},{7,6},{8,11},{9,10},{10,... | collective-permute-start | bytes 1179656 | tf_op jit(solution)/shard_map/ppermute | solution.py:54
  86.5 8.4 %collective-permute-done.16.refs_2_ = bf16[192,512]{1,0:T(8,128)(2,1)S(1)} collective-permute-done((bf16[192,512]{1,0:T(8,128)(2,1)S(1)}, bf16[192,512]{1,0:T(8,128)(2,1)S(1)}, u32[]{:S(2)}, u32[]{:S(2)}) %collective-permute-start.16) | collective-permute-done | bytes 196640 | tf_op jit(solution)/shard_map/ppermute | solution.py:54
  95.7 3.4 %collective-permute-done.19.refs_0_ = bf16[2,192,512]{2,1,0:T(8,128)(2,1)S(1)} collective-permute-done((bf16[2,192,512]{2,1,0:T(8,128)(2,1)S(1)}, bf16[2,192,512]{2,1,0:T(8,128)(2,1)S(1)}, u32[]{:S(2)}, u32[]{:S(2)}) %collective-permute-start.19) | collective-permute-done | bytes 393248 | tf_op jit(solution)/shard_map/ppermute | solution.py:54
  99.1 1.0 shard_map.67.refs_2_
  100.1 11.2 %collective-permute-done.17.refs_0_ = bf16[2,192,512]{2,1,0:T(8,128)(2,1)S(1)} collective-permute-done((bf16[2,192,512]{2,1,0:T(8,128)(2,1)S(1)}, bf16[2,192,512]{2,1,0:T(8,128)(2,1)S(1)}, u32[]{:S(2)}, u32[]{:S(2)}) %collective-permute-start.17) | collective-permute-done | bytes 393248 | tf_op jit(solution)/shard_map/ppermute | solution.py:54
  111.3 1.3 %shard_map.68 = bf16[192,1024]{1,0:T(8,128)(2,1)} custom-call(bf16[2,192,512]{2,1,0:T(8,128)(2,1)S(1)} %collective-permute-done.17.refs_0_, bf16[4096,1024]{1,0:T(8,128)(2,1)S(1)} %bitcast.11, f32[192,1024]{1,0:T(8,128)S(1)} %shard_map.67.refs_2_), custom_call_target="tpu_custom_call" | custom-call | flops 400000000 | bytes 4000000 | tf_op jit(solution)/shard_map/pallas_call | solution.py:239
  (46 shorter events, 6.5 us)
Async XLA Ops:
  0.9 3.6 %collective-permute-start.1 = (bf16[2,192,128]{2,1,0:T(8,128)(2,1)S(1)}, bf16[2,192,128]{2,1,0:T(8,128)(2,1)S(1)}, u32[]{:S(2)}, u32[]{:S(2)}) collective-permute-start(bf16[2,192,128]{2,1,0:T(8,128)(2,1)S(1)} %get-tuple-element.17), channel_id=1, source_target_pairs={{0,128},{4,0},{8,136},{12,8},{16,144},{20,16},{24,152},{28,24},{32... | collective-permute-start | bytes 294920 | tf_op jit(solution)/shard_map/ppermute | solution.py:50
  1.2 3.2 %collective-permute-start = (bf16[2,192,128]{2,1,0:T(8,128)(2,1)S(1)}, bf16[2,192,128]{2,1,0:T(8,128)(2,1)S(1)}, u32[]{:S(2)}, u32[]{:S(2)}) collective-permute-start(bf16[2,192,128]{2,1,0:T(8,128)(2,1)S(1)} %get-tuple-element.18), channel_id=1, source_target_pairs={{0,0},{4,128},{8,8},{12,136},{16,16},{20,144},{24,24},{28,152},{32... | collective-permute-start | bytes 294920 | tf_op jit(solution)/shard_map/ppermute | solution.py:50
  4.5 5.9 %collective-permute-start.5 = (bf16[2,192,128]{2,1,0:T(8,128)(2,1)S(1)}, bf16[2,192,128]{2,1,0:T(8,128)(2,1)S(1)}, u32[]{:S(2)}, u32[]{:S(2)}) collective-permute-start(bf16[2,192,128]{2,1,0:T(8,128)(2,1)S(1)} %pad_maximum_fusion.7), channel_id=1, source_target_pairs={{0,24},{4,100},{8,16},{12,108},{16,8},{20,116},{24,0},{28,124},{32... | collective-permute-start | bytes 294920 | tf_op jit(solution)/shard_map/ppermute | solution.py:50
  7.4 4.7 %collective-permute-start.2 = (bf16[2,192,128]{2,1,0:T(8,128)(2,1)S(1)}, bf16[2,192,128]{2,1,0:T(8,128)(2,1)S(1)}, u32[]{:S(2)}, u32[]{:S(2)}) collective-permute-start(bf16[2,192,128]{2,1,0:T(8,128)(2,1)S(1)} %pad_maximum_fusion.6), channel_id=1, source_target_pairs={{0,8},{4,36},{8,0},{12,44},{16,24},{20,52},{24,16},{28,60},{32,40}... | collective-permute-start | bytes 294920 | tf_op jit(solution)/shard_map/ppermute | solution.py:50
  10.5 5.8 %collective-permute-start.6 = (bf16[4,192,128]{2,1,0:T(8,128)(2,1)S(1)}, bf16[4,192,128]{2,1,0:T(8,128)(2,1)S(1)}, u32[]{:S(2)}, u32[]{:S(2)}) collective-permute-start(bf16[4,192,128]{2,1,0:T(8,128)(2,1)S(1)} %pad_maximum_fusion.5), channel_id=1, source_target_pairs={{0,8},{4,36},{8,0},{12,44},{16,24},{20,52},{24,16},{28,60},{32,40}... | collective-permute-start | bytes 589832 | tf_op jit(solution)/shard_map/ppermute | solution.py:50
  12.1 7.3 %collective-permute-start.3 = (bf16[4,192,128]{2,1,0:T(8,128)(2,1)S(1)}, bf16[4,192,128]{2,1,0:T(8,128)(2,1)S(1)}, u32[]{:S(2)}, u32[]{:S(2)}) collective-permute-start(bf16[4,192,128]{2,1,0:T(8,128)(2,1)S(1)} %pad_maximum_fusion.4), channel_id=1, source_target_pairs={{0,24},{4,100},{8,16},{12,108},{16,8},{20,116},{24,0},{28,124},{32... | collective-permute-start | bytes 589832 | tf_op jit(solution)/shard_map/ppermute | solution.py:50
  16.3 9.1 %collective-permute-start.7 = (bf16[8,192,128]{2,1,0:T(8,128)(2,1)S(1)}, bf16[8,192,128]{2,1,0:T(8,128)(2,1)S(1)}, u32[]{:S(2)}, u32[]{:S(2)}) collective-permute-start(bf16[8,192,128]{2,1,0:T(8,128)(2,1)S(1)} %pad_maximum_fusion.1), channel_id=1, source_target_pairs={{0,96},{4,28},{8,104},{12,20},{16,112},{20,12},{24,120},{28,4},{32... | collective-permute-start | bytes 1179656 | tf_op jit(solution)/shard_map/ppermute | solution.py:50
  19.4 7.9 %collective-permute-start.4 = (bf16[8,192,128]{2,1,0:T(8,128)(2,1)S(1)}, bf16[8,192,128]{2,1,0:T(8,128)(2,1)S(1)}, u32[]{:S(2)}, u32[]{:S(2)}) collective-permute-start(bf16[8,192,128]{2,1,0:T(8,128)(2,1)S(1)} %pad_maximum_fusion), channel_id=1, source_target_pairs={{0,32},{4,12},{8,40},{12,4},{16,48},{20,28},{24,56},{28,20},{32,0}... | collective-permute-start | bytes 1179656 | tf_op jit(solution)/shard_map/ppermute | solution.py:50
  27.3 13.3 %collective-permute-start.9 = (bf16[16,192,128]{2,1,0:T(8,128)(2,1)S(1)}, bf16[16,192,128]{2,1,0:T(8,128)(2,1)S(1)}, u32[]{:S(2)}, u32[]{:S(2)}) collective-permute-start(bf16[16,192,128]{2,1,0:T(8,128)(2,1)S(1)} %constant_dynamic-update-slice_fusion.refs_0_), channel_id=1, source_target_pairs={{0,96},{4,28},{8,104},{12,20},{16,112},{20,12},{24,120},{28,4},{32... | collective-permute-start | bytes 2359304 | tf_op jit(solution)/shard_map/ppermute | solution.py:50
  30.1 12.0 %collective-permute-start.12 = (bf16[16,192,128]{2,1,0:T(8,128)(2,1)S(1)}, bf16[16,192,128]{2,1,0:T(8,128)(2,1)S(1)}, u32[]{:S(2)}, u32[]{:S(2)}) collective-permute-start(bf16[16,192,128]{2,1,0:T(8,128)(2,1)S(1)} %constant_dynamic-update-slice_fusion.5.refs_4_), channel_id=1, source_target_pairs={{0,32},{4,12},{8,40},{12,4},{16,48},{20,28},{24,56},{28,20},{32,0}... | collective-permute-start | bytes 2359304 | tf_op jit(solution)/shard_map/ppermute | solution.py:50
  30.3 18.1 %collective-permute-start.10 = (bf16[16,192,128]{2,1,0:T(8,128)(2,1)S(1)}, bf16[16,192,128]{2,1,0:T(8,128)(2,1)S(1)}, u32[]{:S(2)}, u32[]{:S(2)}) collective-permute-start(bf16[16,192,128]{2,1,0:T(8,128)(2,1)S(1)} %constant_dynamic-update-slice_fusion.refs_0_), channel_id=1, source_target_pairs={{0,4},{4,0},{8,12},{12,8},{16,20},{20,16},{24,28},{28,24},{32,36},... | collective-permute-start | bytes 2359304 | tf_op jit(solution)/shard_map/ppermute | solution.py:50
  30.3 18.1 %collective-permute-start.13 = (bf16[16,192,128]{2,1,0:T(8,128)(2,1)S(1)}, bf16[16,192,128]{2,1,0:T(8,128)(2,1)S(1)}, u32[]{:S(2)}, u32[]{:S(2)}) collective-permute-start(bf16[16,192,128]{2,1,0:T(8,128)(2,1)S(1)} %constant_dynamic-update-slice_fusion.5.refs_4_), channel_id=1, source_target_pairs={{0,4},{4,0},{8,12},{12,8},{16,20},{20,16},{24,28},{28,24},{32,36},... | collective-permute-start | bytes 2359304 | tf_op jit(solution)/shard_map/ppermute | solution.py:50
  40.6 7.8 %collective-permute-start.11 = (bf16[16,192,128]{2,1,0:T(8,128)(2,1)S(1)}, bf16[16,192,128]{2,1,0:T(8,128)(2,1)S(1)}, u32[]{:S(2)}, u32[]{:S(2)}) collective-permute-start(bf16[16,192,128]{2,1,0:T(8,128)(2,1)S(1)} %collective-permute-done.9.refs_1_), channel_id=1, source_target_pairs={{0,4},{4,0},{8,12},{12,8},{16,20},{20,16},{24,28},{28,24},{32,36},... | collective-permute-start | bytes 2359304 | tf_op jit(solution)/shard_map/ppermute | solution.py:50
  42.1 6.3 %collective-permute-start.14 = (bf16[16,192,128]{2,1,0:T(8,128)(2,1)S(1)}, bf16[16,192,128]{2,1,0:T(8,128)(2,1)S(1)}, u32[]{:S(2)}, u32[]{:S(2)}) collective-permute-start(bf16[16,192,128]{2,1,0:T(8,128)(2,1)S(1)} %collective-permute-done.12.refs_5_), channel_id=1, source_target_pairs={{0,4},{4,0},{8,12},{12,8},{16,20},{20,16},{24,28},{28,24},{32,36},... | collective-permute-start | bytes 2359304 | tf_op jit(solution)/shard_map/ppermute | solution.py:50
  42.1 11.4 %collective-permute-start.8 = (bf16[192,512]{1,0:T(8,128)(2,1)S(1)}, bf16[192,512]{1,0:T(8,128)(2,1)S(1)}, u32[]{:S(2)}, u32[]{:S(2)}) collective-permute-start(bf16[192,512]{1,0:T(8,128)(2,1)S(1)} %get-tuple-element.11), channel_id=1, source_target_pairs={{0,252},{4,248},{8,244},{12,240},{16,236},{20,232},{24,228},{28,22... | collective-permute-start | bytes 589832 | tf_op jit(solution)/shard_map/ppermute | solution.py:50
  48.4 46.6 %slice-start = ((s8[8388608]{0:T(1024)(128)(4,1)}), s8[4194304]{0:T(1024)(128)(4,1)S(1)}, s32[]{:S(2)}) async-start(s8[8388608]{0:T(1024)(128)(4,1)} %bitcast.10), calls=%async_computation | async-start | bytes 8388608
  52.2 42.9 %slice-start.1 = ((s8[8388608]{0:T(1024)(128)(4,1)}), s8[4194304]{0:T(1024)(128)(4,1)S(1)}, s32[]{:S(2)}) async-start(s8[8388608]{0:T(1024)(128)(4,1)} %bitcast.10), calls=%async_computation.1 | async-start | bytes 8388608
  71.1 13.3 %collective-permute-start.15 = (bf16[192,512]{1,0:T(8,128)(2,1)S(1)}, bf16[192,512]{1,0:T(8,128)(2,1)S(1)}, u32[]{:S(2)}, u32[]{:S(2)}) collective-permute-start(bf16[192,512]{1,0:T(8,128)(2,1)S(1)} %shard_map.65), channel_id=1, source_target_pairs={{0,252},{4,248},{8,244},{12,240},{16,236},{20,232},{24,228},{28,22... | collective-permute-start | bytes 589832 | tf_op jit(solution)/shard_map/ppermute | solution.py:50
  71.2 13.2 %collective-permute-start.18 = (bf16[192,512]{1,0:T(8,128)(2,1)S(1)}, bf16[192,512]{1,0:T(8,128)(2,1)S(1)}, u32[]{:S(2)}, u32[]{:S(2)}) collective-permute-start(bf16[192,512]{1,0:T(8,128)(2,1)S(1)} %shard_map.64.refs_0_), channel_id=1, source_target_pairs={{0,1},{1,0},{2,3},{3,2},{4,7},{5,6},{6,5},{7,4},{8,9},{9,8},{10,11... | collective-permute-start | bytes 589832 | tf_op jit(solution)/shard_map/ppermute | solution.py:54
  84.4 10.6 %collective-permute-start.16 = (bf16[192,512]{1,0:T(8,128)(2,1)S(1)}, bf16[192,512]{1,0:T(8,128)(2,1)S(1)}, u32[]{:S(2)}, u32[]{:S(2)}) collective-permute-start(bf16[192,512]{1,0:T(8,128)(2,1)S(1)} %collective-permute-done.15.refs_1_), channel_id=1, source_target_pairs={{0,1},{1,0},{2,3},{3,2},{4,7},{5,6},{6,5},{7,4},{8,9},{9,8},{10,11... | collective-permute-start | bytes 589832 | tf_op jit(solution)/shard_map/ppermute | solution.py:54
  84.4 14.7 %collective-permute-start.19 = (bf16[2,192,512]{2,1,0:T(8,128)(2,1)S(1)}, bf16[2,192,512]{2,1,0:T(8,128)(2,1)S(1)}, u32[]{:S(2)}, u32[]{:S(2)}) collective-permute-start(bf16[2,192,512]{2,1,0:T(8,128)(2,1)S(1)} %pad_maximum_fusion.3), channel_id=1, source_target_pairs={{0,3},{1,2},{2,1},{3,0},{4,5},{5,4},{6,7},{7,6},{8,11},{9,10},{10,... | collective-permute-start | bytes 1179656 | tf_op jit(solution)/shard_map/ppermute | solution.py:54
  95.0 16.3 %collective-permute-start.17 = (bf16[2,192,512]{2,1,0:T(8,128)(2,1)S(1)}, bf16[2,192,512]{2,1,0:T(8,128)(2,1)S(1)}, u32[]{:S(2)}, u32[]{:S(2)}) collective-permute-start(bf16[2,192,512]{2,1,0:T(8,128)(2,1)S(1)} %pad_maximum_fusion.2), channel_id=1, source_target_pairs={{0,3},{1,2},{2,1},{3,0},{4,5},{5,4},{6,7},{7,6},{8,11},{9,10},{10,... | collective-permute-start | bytes 1179656 | tf_op jit(solution)/shard_map/ppermute | solution.py:54
